TPU v7x, 32 devices: a whole 2x2x4 slice. The times are simulated.
32 devices in a mesh: slab: 4 (over y, core), pencil: 8 (over z, x).
Axes of the slice: x: 2, y: 2, z: 4, core: 2. Of those that a mesh axis runs over, the one named last changes fastest.
Arguments:
- density: float32 [128, 768, 512], P('pencil', None, 'slab'), may hold values from -6 to 6
- source: float32 [128, 768, 512], P('pencil', None, 'slab'), may hold values from -6 to 8
- coupling: float32 [3], replicated, may hold values from 0.25 to 2, as said below
- width_inverse: float32 [6, 128, 128], replicated, as said below
- height_inverse: float32 [1, 128, 128], replicated, as said below
- depth_inverse: float32 [4, 128, 128], replicated, as said below
Outputs:
- stepped: float32 [128, 768, 512], P('pencil', None, 'slab')
Inputs may be any that keep to these rules, and one draw needn't show every extreme that they name: coupling holds three positive coefficients. `width_inverse`: block i is the inverse of the i-th pivot block of the block LU factorization of the tridiagonal line matrix with diagonal 1 + 2 s and off-diagonals -s, s the matching coupling. `height_inverse`: as for width_inverse, for the height lines. `depth_inverse`: as for width_inverse, for the depth lines.
All inputs are finite; a program needn't handle non-finite values.
Results may differ from a plain program's by a relative error of at most 0.00027.
Values sent between devices are 32-bit elements; how exact they have to be, the bound alone decides.
A program may use at most 128 MiB of HBM per device.

v0:
```python
import jax
import jax.numpy as jnp
from jax import lax
from jax.experimental import pallas as pl
from jax.experimental.pallas import tpu as pltpu
from jax.sharding import PartitionSpec as P

F32, BF16 = jnp.float32, jnp.bfloat16
MESH = pl.DeviceIdType.MESH


def split(value):
    high = value.astype(BF16)
    return high, (value - high.astype(F32)).astype(BF16)


def both(value, axis):
    return jnp.concatenate(split(value), axis=axis)


def dot(a, b, dims):
    return lax.dot_general(a, b, (dims, ((), ())), preferred_element_type=F32)


def ends_of(plane):
    width, depth = plane.shape
    row = lax.broadcasted_iota(jnp.int32, (depth, depth), 0)
    lane = lax.broadcasted_iota(jnp.int32, (depth, depth), 1)
    lines = []
    for column in (0, depth - 1):
        pieces = []
        for start in range(0, width, depth):
            edge = plane[start : start + depth, column : column + 1]
            pieces.append(jnp.sum(jnp.where(row == lane, edge, 0.0), axis=0, keepdims=True))
        lines.append(jnp.concatenate(pieces, axis=1))
    return jnp.concatenate(lines, axis=0)


def rows_of(pieces, width):
    row = lax.broadcasted_iota(jnp.int32, (16, width), 0)
    value = jnp.zeros((16, width), F32)
    for number, piece in enumerate(pieces):
        value = jnp.where(row == number, piece.astype(F32), value)
    return value.astype(BF16)


class Heights:
    def __init__(self, strength, planes, lanes):
        self.shape, self.planes = (1, lanes), planes
        strength = jnp.full(self.shape, strength, F32)
        self.root = (1.0 + 2.0 * strength + jnp.sqrt(1.0 + 4.0 * strength)) * 0.5
        self.log_ratio = jnp.log(strength / self.root)

    def power(self, index):
        return jnp.exp(jnp.full(self.shape, index, jnp.int32).astype(F32) * self.log_ratio)

    def tail(self, index):
        return 1.0 - self.power(2 * (index + 1))

    def pivot(self, index):
        return self.tail(index) / (self.root * self.tail(index + 1))

    def enter(self, device, j):
        base = device * self.planes
        return (
            self.power(j + 1)
            * (self.tail(base) / self.tail(base + self.planes))
            * (self.tail(self.planes - j - 1) / self.tail(0))
        )

    def leave(self, device, j):
        base = device * self.planes
        return self.power(self.planes - j) * (self.tail(base + j) / self.tail(base + self.planes))

    def through(self, device):
        return self.enter(device, self.planes - 1)


def ends_kernel(slabs, group, rho_ref, halo_ref, ends_ref, got_ref, send_sem, recv_sem):
    j = pl.program_id(0)
    me = lax.axis_index("slab")
    nxt, prv = lax.rem(me + 1, slabs), lax.rem(me + slabs - 1, slabs)
    barrier = pltpu.get_barrier_semaphore()

    @pl.when(j == 0)
    def _():
        for peer in (nxt, prv):
            pl.semaphore_signal(barrier, inc=1, device_id={"slab": peer}, device_id_type=MESH)

    for g in range(group):
        pair = ends_of(rho_ref[g])
        ends_ref[0, j * group + g] = pair[0:1]
        ends_ref[1, j * group + g] = pair[1:2]

    @pl.when(j == pl.num_programs(0) - 1)
    def _():
        pl.semaphore_wait(barrier, 2)
        copies = [
            pltpu.make_async_remote_copy(
                src_ref=ends_ref.at[1 - way],
                dst_ref=got_ref.at[way],
                send_sem=send_sem.at[way],
                recv_sem=recv_sem.at[way],
                device_id={"slab": peer},
                device_id_type=MESH,
            )
            for way, peer in ((0, nxt), (1, prv))
        ]
        for copy in copies:
            copy.start()
        for copy in copies:
            copy.wait()
        halo_ref[0] = jnp.where(me == 0, 0.0, got_ref[0])
        halo_ref[1] = jnp.where(me == slabs - 1, 0.0, got_ref[1])


def height_kernel(
    planes, group, coupling, rho_ref, source_ref, halo_ref, x_ref, faces_ref, kept_ref
):
    step = pl.program_id(0)
    width, depth = rho_ref.shape[1:]
    strength = coupling[1]
    row = lax.broadcasted_iota(jnp.int32, (width, depth), 0)
    lane = lax.broadcasted_iota(jnp.int32, (width, depth), 1)
    first = (lax.broadcasted_iota(jnp.int32, (1, depth), 1) == 0).astype(F32)
    last = (lax.broadcasted_iota(jnp.int32, (1, depth), 1) == depth - 1).astype(F32)
    units = rows_of((first, first, last, last), depth)
    heights = Heights(strength, planes, depth)
    base = lax.axis_index("pencil") * planes

    @pl.when(step == 0)
    def _():
        x_ref[planes - 1] = jnp.zeros((width, depth), F32)

    for g in range(group):
        j = step * group + g
        rho = rho_ref[g]
        below = jnp.where(row == 0, 0.0, pltpu.roll(rho, 1, 0))
        above = jnp.where(row == width - 1, 0.0, pltpu.roll(rho, width - 1, 0))
        before = jnp.where(lane == 0, 0.0, pltpu.roll(rho, 1, 1))
        after = jnp.where(lane == depth - 1, 0.0, pltpu.roll(rho, depth - 1, 1))
        left_high, left_low = split(halo_ref[0, g])
        right_high, right_low = split(halo_ref[1, g])
        edge = dot(rows_of((left_high, left_low, right_high, right_low), width), units, ((0,), (0,)))
        rhs = (
            2.0
            * (
                coupling[0] * (below + above - 2.0 * rho)
                + coupling[2] * (before + after + edge - 2.0 * rho)
            )
            + source_ref[g]
            + 2.0 * rho
        )
        kept_ref[j] = 2.0 * rho
        x_ref[j] = (rhs + strength * x_ref[lax.rem(j + planes - 1, planes)]) * heights.pivot(base + j)

    @pl.when(step == planes // group - 1)
    def _():
        shape = faces_ref.shape
        faces_ref[:, 0] = x_ref[planes - 1].reshape(shape[0], shape[2], shape[3])

        def back(count, unused):
            i = planes - 2 - count
            later = x_ref[i + 1]
            x_ref[i] = x_ref[i] + (strength * heights.pivot(base + i)) * later
            x_ref[i + 1] = later - kept_ref[i + 1]
            return unused

        lax.fori_loop(0, planes - 1, back, 0)
        faces_ref[:, 1] = x_ref[0].reshape(shape[0], shape[2], shape[3])
        x_ref[0] = x_ref[0] - kept_ref[0]


def solve_group(rhs, strength, width_ref, mixed_ref, depth_mixed):
    count, size = width_ref.shape[:2]
    depth = size
    total = rhs.shape[1]
    high, low = split(rhs)
    local, starts, stops = [], [], []
    for i in range(count):
        part = slice(i * size, (i + 1) * size)
        product = dot(mixed_ref[i], jnp.concatenate([high[part], low[part]], 0), ((1,), (0,)))
        local.append(product[:size] + product[size:])
        starts.append(strength * width_ref[i, :, 0:1])
        stops.append(strength * width_ref[i, :, size - 1 : size])
    carry = jnp.zeros((1, total), F32)
    ahead, heads = [], []
    for i in range(count):
        ahead.append(carry)
        heads.append(local[i][0:1] + starts[i][0:1] * carry)
        carry = local[i][size - 1 :] + starts[i][size - 1 :] * carry
    carry = jnp.zeros((1, total), F32)
    solved = [None] * count
    for i in reversed(range(count)):
        solved[i] = local[i] + starts[i] * ahead[i] + stops[i] * carry
        carry = heads[i] + stops[i][0:1] * carry
    solved = jnp.concatenate(solved, axis=0)
    answers = []
    for start in range(0, total, depth):
        product = dot(both(solved[:, start : start + depth], 1), depth_mixed, ((1,), (0,)))
        answers.append(product[:, :depth] + product[:, depth:])
    return answers


def lines_kernel(
    group, pencils, slabs,
    coupling,
    u_hbm, faces_ref, width_ref, depth_ref,
    z_hbm, carry_ref,
    u_ref, z_ref, mixed_ref, mixed_depth,
    held, solved, final, face_z, ends, gathered,
    send_one, recv_one, send_two, recv_two, send_three, recv_three, load_sem, store_sem,
):
    planes, width, depth = u_ref.shape
    groups = planes // group
    count, size = width_ref.shape[:2]
    me, slab = lax.axis_index("pencil"), lax.axis_index("slab")
    barrier = pltpu.get_barrier_semaphore()
    for k in range(1, pencils):
        pl.semaphore_signal(
            barrier, inc=1, device_id={"pencil": lax.rem(me + k, pencils)}, device_id_type=MESH
        )
    for k in range(1, slabs):
        pl.semaphore_signal(
            barrier, inc=1, device_id={"slab": lax.rem(slab + k, slabs)}, device_id_type=MESH
        )

    def load(index):
        part = pl.ds(index * group, group)
        return pltpu.make_async_copy(u_hbm.at[part], u_ref.at[part], load_sem.at[index])

    def store(j):
        return pltpu.make_async_copy(z_ref.at[j], z_hbm.at[j], store_sem.at[j])

    for index in range(groups):
        load(index).start()
    for i in range(count):
        high, low = split(width_ref[i])
        mixed_ref[i, :size, :size] = high
        mixed_ref[i, :size, size:] = high
        mixed_ref[i, size:, :size] = low
        mixed_ref[i, size:, size:] = jnp.zeros_like(low)
    high, low = split(depth_ref[slab])
    mixed_depth[:size, :size] = high
    mixed_depth[size:, :size] = high
    mixed_depth[:size, size:] = low
    mixed_depth[size:, size:] = jnp.zeros_like(low)
    pl.semaphore_wait(barrier, pencils + slabs - 2)
    heights = Heights(coupling[1], planes, depth)

    def exchange(source, target, send, recv):
        copies = []
        for k in range(1, pencils):
            peer = lax.rem(me + k, pencils)
            copy = pltpu.make_async_remote_copy(
                src_ref=source.at[peer],
                dst_ref=target.at[me],
                send_sem=send.at[k - 1],
                recv_sem=recv.at[k - 1],
                device_id={"pencil": peer},
                device_id_type=MESH,
            )
            copy.start()
            copies.append(copy)
        target[me] = source[me]
        return copies

    def some(begin, end):
        def body(index, unused):
            base = index * group
            load(index).wait()
            rhs = jnp.concatenate([u_ref[base + g] for g in range(group)], axis=1)
            answers = solve_group(rhs, coupling[0], width_ref, mixed_ref, mixed_depth[...])
            for g in range(group):
                z_ref[base + g] = answers[g]
                ends[base + g] = ends_of(answers[g])
            return unused

        lax.fori_loop(begin, end, body, 0)

    copies = exchange(faces_ref, held, send_one, recv_one)
    some(0, groups // 2)
    for copy in copies:
        copy.wait()
    value = jnp.zeros(held.shape[2:], F32)
    for d in range(pencils):
        solved[d, 0] = value
        if d < pencils - 1:
            value = held[d, 0] + heights.through(d) * value
    value = jnp.zeros(held.shape[2:], F32)
    for d in reversed(range(pencils)):
        solved[d, 1] = value
        if d > 0:
            value = held[d, 1] + heights.enter(d, 0) * solved[d, 0] + heights.leave(d, 0) * value
    copies = exchange(solved, final, send_two, recv_two)
    some(groups // 2, groups)
    for copy in copies:
        copy.wait()
    rhs = jnp.concatenate([final[:, side].reshape(width, depth) for side in range(2)], axis=1)
    answers = solve_group(rhs, coupling[0], width_ref, mixed_ref, mixed_depth[...])
    for side in range(2):
        face_z[side] = answers[side]
    edge_enter, edge_leave = ends_of(answers[0]), ends_of(answers[1])

    def correct_ends(j, unused):
        enter, leave = heights.enter(me, j)[:, 0:1], heights.leave(me, j)[:, 0:1]
        ends[j] = ends[j] + enter * edge_enter + leave * edge_leave
        return unused

    def correct(j, unused):
        enter, leave = heights.enter(me, j), heights.leave(me, j)
        z_ref[j] = z_ref[j] + enter * face_z[0] + leave * face_z[1]
        store(j).start()
        return unused

    def finish_store(j, unused):
        store(j).wait()
        return unused

    lax.fori_loop(0, planes, correct_ends, 0)
    copies = []
    for k in range(1, slabs):
        copy = pltpu.make_async_remote_copy(
            src_ref=ends,
            dst_ref=gathered.at[slab],
            send_sem=send_three.at[k - 1],
            recv_sem=recv_three.at[k - 1],
            device_id={"slab": lax.rem(slab + k, slabs)},
            device_id_type=MESH,
        )
        copy.start()
        copies.append(copy)
    gathered[slab] = ends[...]
    lax.fori_loop(0, planes, correct, 0)
    for copy in copies:
        copy.wait()

    def link(d, row, column):
        return coupling[2] * depth_ref[d, row : row + 1, column : column + 1]

    zero = jnp.zeros((planes, width), F32)
    forward = [zero]
    for d in range(slabs - 1):
        forward.append(gathered[d, :, 1] + link(d, size - 1, 0) * forward[d])
    backward = [zero] * slabs
    for d in range(slabs - 1, 0, -1):
        backward[d - 1] = (
            gathered[d, :, 0] + link(d, 0, 0) * forward[d] + link(d, 0, size - 1) * backward[d]
        )
    carry_in, carry_next = forward[0], backward[0]
    for d in range(1, slabs):
        carry_in = jnp.where(slab == d, forward[d], carry_in)
        carry_next = jnp.where(slab == d, backward[d], carry_next)
    carry_ref[:, 0] = carry_in
    carry_ref[:, 1] = carry_next
    lax.fori_loop(0, planes, finish_store, 0)


def finish_kernel(group, coupling, rho_ref, z_ref, carry_ref, depth_ref, out_ref):
    width, depth = rho_ref.shape[1:]
    slab, size = lax.axis_index("slab"), depth_ref.shape[1]
    in_high, in_low = split(coupling[2] * depth_ref[slab, 0:1])
    next_high, next_low = split(coupling[2] * depth_ref[slab, size - 1 : size])
    rhs = rows_of((in_high, in_high, in_low, next_high, next_high, next_low), depth)
    for g in range(group):
        a_high, a_low = split(carry_ref[g, 0:1])
        b_high, b_low = split(carry_ref[g, 1:2])
        lhs = rows_of((a_high, a_low, a_high, b_high, b_low, b_high), width)
        out_ref[g] = rho_ref[g] + z_ref[g] + dot(lhs, rhs, ((0,), (0,)))


def per_device(density, source, coupling, width_inverse, height_inverse, depth_inverse):
    planes, width, depth = density.shape
    pencils, slabs = lax.axis_size("pencil"), lax.axis_size("slab")
    size = depth_inverse.shape[1]
    group = 2
    smem = pl.BlockSpec(memory_space=pltpu.SMEM)
    params = pltpu.CompilerParams(
        dimension_semantics=("arbitrary",), vmem_limit_bytes=56 * 1024 * 1024
    )

    def whole(shape):
        return pl.BlockSpec(shape, lambda j: (0,) * len(shape))

    def per_plane(shape):
        return pl.BlockSpec(shape, lambda j: (j,) + (0,) * (len(shape) - 1))

    def plane_pairs(shape):
        return pl.BlockSpec(shape, lambda j: (0, j, 0, 0))

    vmem = pl.BlockSpec(memory_space=pltpu.VMEM)
    hbm = pl.BlockSpec(memory_space=pl.ANY)
    blocks = width_inverse.shape[0]
    dma = pltpu.SemaphoreType.DMA
    strip = (2, planes, 1, width)
    halo = pl.pallas_call(
        lambda *refs: ends_kernel(slabs, 4, *refs),
        grid=(planes // 4,),
        out_shape=jax.ShapeDtypeStruct(strip, F32),
        in_specs=[per_plane((4, width, depth))],
        out_specs=whole(strip),
        scratch_shapes=[pltpu.VMEM(strip, F32), pltpu.VMEM(strip, F32), dma((2,)), dma((2,))],
        compiler_params=pltpu.CompilerParams(
            dimension_semantics=("arbitrary",),
            vmem_limit_bytes=56 * 1024 * 1024,
            collective_id=0,
            has_side_effects=True,
        ),
    )(density)

    share = width // pencils
    partial, faces = pl.pallas_call(
        lambda *refs: height_kernel(planes, group, *refs),
        grid=(planes // group,),
        out_shape=(
            jax.ShapeDtypeStruct((planes, width, depth), F32),
            jax.ShapeDtypeStruct((pencils, 2, share, depth), F32),
        ),
        in_specs=[
            smem,
            per_plane((group, width, depth)),
            per_plane((group, width, depth)),
            plane_pairs((2, group, 1, width)),
        ],
        out_specs=(whole((planes, width, depth)), whole((pencils, 2, share, depth))),
        scratch_shapes=[pltpu.VMEM((planes, width, depth), F32)],
        compiler_params=params,
    )(coupling, density, source, halo)

    pieces = pltpu.VMEM((pencils, 2, share, depth), F32)
    local, carries = pl.pallas_call(
        lambda *refs: lines_kernel(group, pencils, slabs, *refs),
        out_shape=(
            jax.ShapeDtypeStruct((planes, width, depth), F32),
            jax.ShapeDtypeStruct((planes, 2, width), F32),
        ),
        in_specs=[smem, hbm, vmem, vmem, vmem],
        out_specs=(hbm, vmem),
        scratch_shapes=[
            pltpu.VMEM((planes, width, depth), F32),
            pltpu.VMEM((planes, width, depth), F32),
            pltpu.VMEM((blocks, 2 * size, 2 * size), BF16),
            pltpu.VMEM((2 * size, 2 * size), BF16),
            pieces,
            pieces,
            pieces,
            pltpu.VMEM((2, width, depth), F32),
            pltpu.VMEM((planes, 2, width), F32),
            pltpu.VMEM((slabs, planes, 2, width), F32),
            dma((pencils - 1,)),
            dma((pencils - 1,)),
            dma((pencils - 1,)),
            dma((pencils - 1,)),
            dma((slabs - 1,)),
            dma((slabs - 1,)),
            dma((planes // group,)),
            dma((planes,)),
        ],
        compiler_params=pltpu.CompilerParams(
            vmem_limit_bytes=56 * 1024 * 1024, collective_id=1, has_side_effects=True
        ),
    )(coupling, partial, faces, width_inverse, depth_inverse)

    return pl.pallas_call(
        lambda *refs: finish_kernel(group, *refs),
        grid=(planes // group,),
        out_shape=jax.ShapeDtypeStruct((planes, width, depth), F32),
        in_specs=[
            smem,
            per_plane((group, width, depth)),
            per_plane((group, width, depth)),
            per_plane((group, 2, width)),
            whole(depth_inverse.shape),
        ],
        out_specs=per_plane((group, width, depth)),
        compiler_params=params,
    )(coupling, density, local, carries, depth_inverse)


def solution(mesh):
    in_specs = (P("pencil", None, "slab"), P("pencil", None, "slab"), P(), P(), P(), P())
    out_specs = P("pencil", None, "slab")
    return jax.shard_map(
        per_device, mesh=mesh, in_specs=in_specs, out_specs=out_specs, check_vma=False
    )
```

profile of v0, /device:TPU:31, one launch (start us, length us, event | category | flops | bytes accessed | tf_op | source)
XLA Modules:
  0.0 85.2 jit_solution(13938588698687344015)
XLA Ops:
  0.0 8.9 %shard_map.55.refs_3_ = f32[2,16,1,768]{3,2,1,0:T(1,128)} custom-call(f32[16,768,128]{2,1,0:T(8,128)} %refs_1_.3), custom_call_target="tpu_custom_call" | custom-call | tf_op jit(solution)/shard_map/pallas_call | solution.py:396
  8.9 15.1 %shard_map.56 = (f32[16,768,128]{2,1,0:T(8,128)}, f32[8,2,96,128]{3,2,1,0:T(8,128)}) custom-call(f32[3]{0:T(128)} %refs_0_.7, f32[16,768,128]{2,1,0:T(8,128)} %refs_1_.3, f32[16,768,128]{2,1,0:T(8,128)} %refs_2_.1, f32[2,16,1,768]{3,2,1,0:T(1,128)} %shard_map.55.refs_3_), custom_call_target="tpu_custom_call" | custom-call | tf_op jit(solution)/shard_map/pallas_call | solution.py:412
  24.0 50.6 %shard_map.57 = (f32[16,768,128]{2,1,0:T(8,128)}, f32[16,2,768]{2,1,0:T(2,128)}) custom-call(f32[3]{0:T(128)} %refs_0_.7, f32[16,768,128]{2,1,0:T(8,128)} %get-tuple-element.9.refs_1_, f32[8,2,96,128]{3,2,1,0:T(8,128)} %get-tuple-element.10.refs_2_, f32[6,128,128]{2,1,0:T(8,128)} %refs_3_.1, f32[4,128,128]{2,1,0:T(8,128)} %refs_4_.3), custom_call_target="tpu_custom_call" | custom-call | tf_op jit(solution)/shard_map/pallas_call | solution.py:431
  74.6 10.6 %shard_map.58 = f32[16,768,128]{2,1,0:T(8,128)} custom-call(f32[3]{0:T(128)} %refs_0_.7, f32[16,768,128]{2,1,0:T(8,128)} %refs_1_.3, f32[16,768,128]{2,1,0:T(8,128)} %get-tuple-element.11.refs_2_, f32[16,2,768]{2,1,0:T(2,128)} %get-tuple-element.12.refs_3_, f32[4,128,128]{2,1,0:T(8,128)} %refs_4_.3), custom_call_target="tpu_custom_call" | custom-call | tf_op jit(solution)/shard_map/pallas_call | solution.py:464
where the time goes:
time: 85.7 us; the launch traced here: 85.2 us
  Pallas kernels  85.2 us (99%)
    pallas_call x1, Pallas kernels, per_device(): pl.pallas_call(lambda *refs: lines_kernel(group, pencils, slabs, *refs),...  50.6 us
    pallas_call x1, Pallas kernels, per_device(): pl.pallas_call(lambda *refs: height_kernel(planes, group, *refs), grid=(p...  15.1 us
    pallas_call x1, Pallas kernels, per_device(): pl.pallas_call(lambda *refs: finish_kernel(group, *refs), grid=(planes //...  10.6 us
    pallas_call x1, Pallas kernels, per_device(): pl.pallas_call(lambda *refs: ends_kernel(slabs, 4, *refs), grid=(planes /...  8.91 us

commit v1 on v0

v1 whole, which is shorter than its diff:
```python
import jax
import jax.numpy as jnp
from jax import lax
from jax.experimental import pallas as pl
from jax.experimental.pallas import tpu as pltpu
from jax.sharding import PartitionSpec as P

F32, BF16 = jnp.float32, jnp.bfloat16
MESH = pl.DeviceIdType.MESH


def split(value):
    high = value.astype(BF16)
    return high, (value - high.astype(F32)).astype(BF16)


def both(value, axis):
    return jnp.concatenate(split(value), axis=axis)


def dot(a, b, dims):
    return lax.dot_general(a, b, (dims, ((), ())), preferred_element_type=F32)


def ends_of(plane):
    width, depth = plane.shape
    row = lax.broadcasted_iota(jnp.int32, (depth, depth), 0)
    lane = lax.broadcasted_iota(jnp.int32, (depth, depth), 1)
    lines = []
    for column in (0, depth - 1):
        pieces = []
        for start in range(0, width, depth):
            edge = plane[start : start + depth, column : column + 1]
            pieces.append(jnp.sum(jnp.where(row == lane, edge, 0.0), axis=0, keepdims=True))
        lines.append(jnp.concatenate(pieces, axis=1))
    return jnp.concatenate(lines, axis=0)


def rows_of(pieces, width):
    row = lax.broadcasted_iota(jnp.int32, (16, width), 0)
    value = jnp.zeros((16, width), F32)
    for number, piece in enumerate(pieces):
        value = jnp.where(row == number, piece.astype(F32), value)
    return value.astype(BF16)


def solve_group(rhs, strength, width_ref, mixed_ref, depth_mixed):
    count, size = width_ref.shape[:2]
    depth = size
    total = rhs.shape[1]
    high, low = split(rhs)
    local, starts, stops = [], [], []
    for i in range(count):
        part = slice(i * size, (i + 1) * size)
        product = dot(mixed_ref[i], jnp.concatenate([high[part], low[part]], 0), ((1,), (0,)))
        local.append(product[:size] + product[size:])
        starts.append(strength * width_ref[i, :, 0:1])
        stops.append(strength * width_ref[i, :, size - 1 : size])
    carry = jnp.zeros((1, total), F32)
    ahead, heads = [], []
    for i in range(count):
        ahead.append(carry)
        heads.append(local[i][0:1] + starts[i][0:1] * carry)
        carry = local[i][size - 1 :] + starts[i][size - 1 :] * carry
    carry = jnp.zeros((1, total), F32)
    solved = [None] * count
    for i in reversed(range(count)):
        solved[i] = local[i] + starts[i] * ahead[i] + stops[i] * carry
        carry = heads[i] + stops[i][0:1] * carry
    solved = jnp.concatenate(solved, axis=0)
    answers = []
    for start in range(0, total, depth):
        product = dot(both(solved[:, start : start + depth], 1), depth_mixed, ((1,), (0,)))
        answers.append(product[:, :depth] + product[:, depth:])
    return answers


class Heights:
    def __init__(self, strength, lanes):
        self.shape = (1, lanes)
        self.strength = jnp.full(self.shape, strength, F32)
        root = (1.0 + 2.0 * self.strength + jnp.sqrt(1.0 + 4.0 * self.strength)) * 0.5
        self.log_ratio = jnp.log(self.strength / root)

    def power(self, index):
        return jnp.exp(jnp.full(self.shape, index, jnp.int32).astype(F32) * self.log_ratio)

    def tail(self, count):
        return 1.0 - self.power(2 * count)

    def beside(self, count):
        return self.power(1) * self.tail(count) / self.tail(count + 1)

    def enter(self, count, j):
        return self.power(j + 1) * self.tail(count - j) / self.tail(count + 1)


def rows_solve(pieces, strength, width_ref, mixed_ref):
    count, size = width_ref.shape[:2]
    local = []
    for i in range(count):
        product = dot(both(pieces[i], 1), mixed_ref[i], ((1,), (1,)))
        local.append(product[:, :size] + product[:, size:])
    carry = jnp.zeros((pieces[0].shape[0], 1), F32)
    ahead, heads = [], []
    for i in range(count):
        start = strength * width_ref[i, 0:1]
        ahead.append(start * carry)
        heads.append(local[i][:, 0:1] + start[:, 0:1] * carry)
        carry = local[i][:, size - 1 :] + start[:, size - 1 :] * carry
    carry = jnp.zeros((pieces[0].shape[0], 1), F32)
    solved = [None] * count
    for i in reversed(range(count)):
        stop = strength * width_ref[i, size - 1 : size]
        solved[i] = local[i] + ahead[i] + stop * carry
        carry = heads[i] + stop[:, 0:1] * carry
    return solved


def step_kernel(
    group, pencils, slabs, chunk,
    coupling,
    rho_hbm, source_hbm, width_ref, depth_ref,
    z_ref, face_ref, coef_ref,
    rho_ref, source_ref, y_ref, mixed_ref, mixed_depth,
    pair_out, pair_in, block, up_out, up_in, down_out, down_in, back_out, final,
    ends, gathered, carries, late, late_in,
    load_sem, pair_send, pair_recv, up_send, up_recv, down_send, down_recv,
    back_send, back_recv, early_send, early_recv, late_send, late_recv,
):
    planes, width, depth = z_ref.shape
    groups = planes // group
    count, size = width_ref.shape[:2]
    half = width // 2
    seg = final.shape[1] // 2
    extra = seg - half
    chunks = seg // chunk
    strips = half // depth
    pad = 8
    me, slab = lax.axis_index("pencil"), lax.axis_index("slab")
    outer = pencils // 2
    z, x = lax.div(me, 2), lax.rem(me, 2)
    pair = z * 2 + 1 - x
    above_me = lax.rem(me + 2, pencils)
    below_me = lax.rem(me + pencils - 2, pencils)

    barrier = pltpu.get_barrier_semaphore()
    for peer in (pair, above_me, below_me):
        pl.semaphore_signal(barrier, inc=1, device_id={"pencil": peer}, device_id_type=MESH)
    for k in range(1, slabs):
        pl.semaphore_signal(
            barrier, inc=1, device_id={"slab": lax.rem(slab + k, slabs)}, device_id_type=MESH
        )

    loads = {}

    def load(key, src, dst, start, rows, shift):
        number = loads.setdefault(key, len(loads))
        return pltpu.make_async_copy(
            src.at[:, pl.ds(pl.multiple_of(start, 8), rows)],
            dst.at[:, pl.ds(pl.multiple_of(start + shift, 8), rows)],
            load_sem.at[number],
        )

    def rim(h, side):
        start = h * half + side * (half - 8)
        return load(("rim", h, side), rho_hbm, rho_ref, start, 8, pad)

    def main(turn, h, piece):
        low = 8 if piece == 0 else piece * depth
        high = half - 8 if piece == strips - 1 else (piece + 1) * depth
        return load(("rho", turn, piece), rho_hbm, rho_ref, h * half + low, high - low, pad)

    def other(turn, h, piece):
        start = h * half + piece * depth
        return load(("source", turn, piece), source_hbm, source_ref, start, depth, 0)

    for h in (0, 1):
        for side in (0, 1):
            rim(h, side).start()
    for turn, h in ((0, 1 - x), (1, x)):
        for piece in range(strips):
            main(turn, h, piece).start()
            other(turn, h, piece).start()

    rho_ref[:, :pad] = jnp.zeros((planes, pad, depth), F32)
    rho_ref[:, pad + width :] = jnp.zeros((planes, pad, depth), F32)
    for i in range(count):
        high, low = split(width_ref[i])
        mixed_ref[i, :size, :size] = high
        mixed_ref[i, :size, size:] = high
        mixed_ref[i, size:, :size] = low
        mixed_ref[i, size:, size:] = jnp.zeros_like(low)
    high, low = split(depth_ref[slab])
    mixed_depth[:size, :size] = high
    mixed_depth[size:, :size] = high
    mixed_depth[:size, size:] = low
    mixed_depth[size:, size:] = jnp.zeros_like(low)

    heights = Heights(coupling[1], depth)
    for j in range(planes):
        coef_ref[j : j + 1] = heights.enter(planes, j)
    strength = heights.strength
    ahead = [heights.beside(j + 1) for j in range(planes)]
    pivot = [value / strength for value in ahead]
    near, far = heights.enter(planes, 0), heights.enter(planes, planes - 1)
    gain = 1.0 / (1.0 - near * near)
    near2, far2 = heights.enter(2 * planes, 0), heights.enter(2 * planes, 2 * planes - 1)
    under = heights.beside(2 * planes * z)
    over = heights.beside(2 * planes * (outer - 1 - z))
    under_gain, over_gain = 1.0 / (1.0 - under * near2), 1.0 / (1.0 - over * near2)
    det = 1.0 / ((1.0 - under * near2) * (1.0 - over * near2) - under * over * far2 * far2)
    k_uu, k_uo = (1.0 - over * near2) * det, under * far2 * det
    k_oo, k_ou = (1.0 - under * near2) * det, over * far2 * det

    lane = lax.broadcasted_iota(jnp.int32, (1, depth), 1)
    across, along = coupling[0], coupling[2]
    k_here = 2.0 - 4.0 * across - 4.0 * along
    k_before = jnp.where(lane == 0, 0.0, jnp.full((1, depth), 2.0 * along, F32))
    k_after = jnp.where(lane == depth - 1, 0.0, jnp.full((1, depth), 2.0 * along, F32))

    def back_sweep(at, value):
        for j in reversed(range(planes)):
            if j == planes - 1:
                y = pivot[j] * value
            else:
                y = pivot[j] * (y_ref[j, at] + strength * y)
            y_ref[j, at] = y
        return y

    def sweep(h, row, rows):
        base = pl.multiple_of(pad + h * half + row, 8)
        at = pl.ds(pl.multiple_of(h * seg + row, 8), rows)
        from_source = pl.ds(pl.multiple_of(h * half + row, 8), rows)
        value = None
        for j in range(planes):
            rho = rho_ref[j, pl.ds(base, rows)]
            beside = rho_ref[j, pl.ds(base - 1, rows)] + rho_ref[j, pl.ds(base + 1, rows)]
            rhs = (
                source_ref[j, from_source]
                + k_here * rho
                + (2.0 * across) * beside
                + k_before * pltpu.roll(rho, 1, 1)
                + k_after * pltpu.roll(rho, depth - 1, 1)
            )
            value = rhs if j == 0 else rhs + ahead[j - 1] * value
            y_ref[j, at] = value
        last = pivot[planes - 1] * value
        first = back_sweep(at, value)
        return first, last

    def edge_sweep(h):
        at = pl.ds(pl.multiple_of(h * seg + half, 8), extra)
        value = None
        row = lax.broadcasted_iota(jnp.int32, (depth, depth), 0)
        column = lax.broadcasted_iota(jnp.int32, (depth, depth), 1)

        def gather(j, unused):
            lines = []
            for edge in (0, depth - 1):
                for strip in range(strips):
                    start = pl.multiple_of(pad + h * half + strip * depth, 8)
                    piece = rho_ref[j, pl.ds(start, depth)][:, edge : edge + 1]
                    lines.append(jnp.sum(jnp.where(row == column, piece, 0.0), axis=0, keepdims=True))
            lines.append(jnp.zeros((extra - 2 * strips, depth), F32))
            y_ref[j, at] = jnp.concatenate(lines, axis=0)
            return unused

        lax.fori_loop(0, planes, gather, 0)
        for j in range(planes):
            rhs = y_ref[j, at]
            value = rhs if j == 0 else rhs + ahead[j - 1] * value
            y_ref[j, at] = value
        last = pivot[planes - 1] * value
        first = back_sweep(at, value)
        return first, last

    def remote(source, target, send, recv, peer, axis="pencil"):
        return pltpu.make_async_remote_copy(
            src_ref=source, dst_ref=target, send_sem=send, recv_sem=recv,
            device_id={axis: peer}, device_id_type=MESH,
        )

    def rows_at(c, shift=0):
        return pl.ds(pl.multiple_of(c * chunk + shift, 8), chunk)

    def to_pair(c):
        at = rows_at(c)
        return remote(
            pair_out.at[:, at], pair_in.at[:, at], pair_send.at[c], pair_recv.at[c], pair
        )

    def to_above(c):
        at = rows_at(c)
        return remote(up_out.at[at], up_in.at[at], up_send.at[c], up_recv.at[c], above_me)

    def to_below(c):
        at = rows_at(c)
        return remote(
            down_out.at[at], down_in.at[at], down_send.at[c], down_recv.at[c], below_me
        )

    def to_back(c):
        return remote(
            back_out.at[:, rows_at(c)], final.at[:, rows_at(c, x * seg)],
            back_send.at[c], back_recv.at[c], pair,
        )

    for turn, h in ((0, 1 - x), (1, x)):
        if turn == 0:
            for hh in (0, 1):
                for side in (0, 1):
                    rim(hh, side).wait()
        ready = 0
        for c in range(chunks):
            need = min(strips, -(-(c * chunk + chunk + 1) // depth))
            while ready < need:
                main(turn, h, ready).wait()
                other(turn, h, ready).wait()
                ready += 1
            row = c * chunk
            at = pl.ds(row, min(chunk, half - row))
            first, last = sweep(h, row, min(chunk, half - row))
            if turn == 0:
                pair_out[0, at] = first
                pair_out[1, at] = last
            if c == chunks - 1:
                at = pl.ds(half, extra)
                first, last = edge_sweep(h)
                if turn == 0:
                    pair_out[0, at] = first
                    pair_out[1, at] = last
            if turn == 0:
                if c == 0:
                    pl.semaphore_wait(barrier, 3 + slabs - 1)
                to_pair(c).start()

    @pl.when(z == 0)
    def _():
        up_in[...] = jnp.zeros_like(up_in)

    @pl.when(z == outer - 1)
    def _():
        down_in[...] = jnp.zeros_like(down_in)

    def faces_of(c):
        at, mine = rows_at(c), rows_at(c, x * seg)
        own_first, own_last = y_ref[0, mine], y_ref[planes - 1, mine]
        its_first, its_last = pair_in[0, at], pair_in[1, at]
        lower = x == 0
        return (
            jnp.where(lower, own_first, its_first),
            jnp.where(lower, own_last, its_last),
            jnp.where(lower, its_first, own_first),
            jnp.where(lower, its_last, own_last),
        )

    def do_pair(c):
        to_pair(c).wait_recv()
        at = rows_at(c)
        f0, l0, f1, l1 = faces_of(c)
        block[0, at] = f0 + far * gain * (f1 + near * l0)
        block[1, at] = l1 + far * gain * (l0 + near * f1)

    def do_up(c):
        @pl.when(z > 0)
        def _():
            to_above(c).wait_recv()

        at = rows_at(c)

        @pl.when(z < outer - 1)
        def _():
            up_out[at] = block[1, at] + far2 * under_gain * (up_in[at] + under * block[0, at])
            to_above(c).start()

    def do_down(c):
        @pl.when(z < outer - 1)
        def _():
            to_below(c).wait_recv()

        at = rows_at(c)

        @pl.when(z > 0)
        def _():
            down_out[at] = block[0, at] + far2 * over_gain * (down_in[at] + over * block[1, at])
            to_below(c).start()

    def do_final(c):
        at, mine = rows_at(c), rows_at(c, x * seg)
        low = up_in[at] + under * block[0, at]
        high = down_in[at] + over * block[1, at]
        enter = k_uu * low + k_uo * high
        leave = k_ou * low + k_oo * high
        f0, l0, f1, l1 = faces_of(c)
        l0 = l0 + far * enter
        f1 = f1 + far * leave
        inner_low = gain * (l0 + near * f1)
        inner_high = gain * (f1 + near * l0)
        lower = x == 0
        final[0, mine] = jnp.where(lower, enter, inner_low)
        final[1, mine] = jnp.where(lower, inner_high, leave)
        back_out[0, at] = jnp.where(lower, inner_low, enter)
        back_out[1, at] = jnp.where(lower, leave, inner_high)
        to_back(c).start()

    def blocks_at(i):
        return pl.ds(i // strips * seg + i % strips * size, size)

    def solve_planes(index):
        base = index * group
        rhs = jnp.concatenate(
            [
                jnp.concatenate(
                    [
                        y_ref[base + g, blocks_at(i)]
                        - 2.0 * rho_ref[base + g, pl.ds(pad + i * size, size)]
                        for i in range(count)
                    ],
                    axis=0,
                )
                for g in range(group)
            ],
            axis=1,
        )
        answers = solve_group(rhs, coupling[0], width_ref, mixed_ref, mixed_depth[...])
        for g in range(group):
            z_ref[base + g] = answers[g] + rho_ref[base + g, pl.ds(pad, width)]
            lines = ends_of(answers[g])
            ends[0, pl.ds(base + g, 1)] = lines[0:1]
            ends[1, pl.ds(base + g, 1)] = lines[1:2]

    before_me = jnp.where(slab > 0, slab - 1, 0)
    corner = depth_ref[before_me, size - 1 : size, size - 1 : size]
    corner = jnp.where(slab > 0, corner, jnp.zeros_like(corner))

    def link(d, row, column):
        return coupling[2] * depth_ref[d, row : row + 1, column : column + 1]

    def with_edges(edge, ends_value, v_first, v_own):
        row = 0 if edge == 0 else size - 1
        return ends_value + 2.0 * v_own + (2.0 * coupling[2] * corner * link(slab, row, 0)) * v_first

    def early_edges():
        pieces = []
        for i in range(count):
            h, strip = i // strips, i % strips
            rows = [
                y_ref[:, h * seg + half + edge * strips + strip, :] for edge in (0, 1)
            ]
            pieces.append(jnp.concatenate(rows, axis=0))
        value = jnp.concatenate(rows_solve(pieces, coupling[0], width_ref, mixed_ref), axis=1)
        first, last = value[:planes], value[planes:]
        carries[0] = first
        ends[0] = with_edges(0, ends[0], first, first)
        ends[1] = with_edges(1, ends[1], first, last)
        for k in range(1, slabs):
            early(k).start()
        gathered[slab] = ends[...]

    def early(k):
        return remote(
            ends, gathered.at[slab], early_send.at[k - 1], early_recv.at[k - 1],
            lax.rem(slab + k, slabs), "slab",
        )

    def last_link(k):
        return remote(
            late.at[pl.ds(0, 4)], late_in.at[slab, pl.ds(0, 4)],
            late_send.at[k - 1], late_recv.at[k - 1],
            lax.rem(slab + k, slabs), "slab",
        )

    def chain(first_of, last_of, v_first):
        zero = jnp.zeros_like(v_first)
        forward = [zero]
        for d in range(slabs - 1):
            forward.append(last_of(d) + link(d, size - 1, 0) * forward[d])
        backward = [zero] * slabs
        for d in range(slabs - 1, 0, -1):
            backward[d - 1] = (
                first_of(d) + link(d, 0, 0) * forward[d] + link(d, 0, size - 1) * backward[d]
            )
        carry_in, carry_next = forward[0], backward[0]
        for d in range(1, slabs):
            carry_in = jnp.where(slab == d, forward[d], carry_in)
            carry_next = jnp.where(slab == d, backward[d], carry_next)
        return carry_in + (2.0 * coupling[2] * corner) * v_first, carry_next

    def spread(carry_in, carry_next):
        in_high, in_low = split(coupling[2] * depth_ref[slab, 0:1])
        next_high, next_low = split(coupling[2] * depth_ref[slab, size - 1 : size])
        rhs = rows_of((in_high, in_high, in_low, next_high, next_high, next_low), depth)
        a_high, a_low = split(carry_in)
        b_high, b_low = split(carry_next)
        lhs = rows_of((a_high, a_low, a_high, b_high, b_low, b_high), width)
        return dot(lhs, rhs, ((0,), (0,)))

    per_tick = 2
    busy = -(-groups // per_tick)
    ticks = max(chunks + outer - 1, busy + 1)

    def tick(t, unused):
        @pl.when(t < chunks)
        def _():
            do_pair(t)

        up = t - z

        @pl.when((up >= 0) & (up < chunks))
        def _():
            do_up(up)

        down = t - (outer - 1 - z)

        @pl.when((down >= 0) & (down < chunks))
        def _():
            do_down(down)

        done = t - jnp.maximum(z, outer - 1 - z)

        @pl.when((done >= 0) & (done < chunks))
        def _():
            do_final(done)

        @pl.when(t < busy)
        def _():
            def one(k, same):
                solve_planes(t * per_tick + k)
                return same

            lax.fori_loop(0, per_tick, one, 0)

        @pl.when(t == busy)
        def _():
            early_edges()

        return unused

    lax.fori_loop(0, ticks, tick, 0)

    for k in range(1, slabs):
        early(k).wait()
    carry_in, carry_next = chain(
        lambda d: gathered[d, 0], lambda d: gathered[d, 1], carries[0]
    )
    carries[0] = carry_in
    carries[1] = carry_next

    def finish_plane(j, unused):
        z_ref[j] = z_ref[j] + spread(carries[0, pl.ds(j, 1)], carries[1, pl.ds(j, 1)])
        return unused

    lax.fori_loop(0, planes, finish_plane, 0)

    def wait_back(c, unused):
        to_back(c).wait()
        return unused

    lax.fori_loop(0, chunks, wait_back, 0)
    rhs = jnp.concatenate(
        [
            jnp.concatenate([final[side, blocks_at(i)] for i in range(count)], axis=0)
            for side in range(2)
        ],
        axis=1,
    )
    answers = solve_group(rhs, coupling[0], width_ref, mixed_ref, mixed_depth[...])
    pieces = []
    for i in range(count):
        h, strip = i // strips, i % strips
        rows = [
            final[side, h * seg + half + edge * strips + strip, :].reshape(1, depth)
            for edge in (0, 1) for side in (0, 1)
        ]
        rows.append(jnp.zeros((4, depth), F32))
        pieces.append(jnp.concatenate(rows, axis=0))
    value = jnp.concatenate(rows_solve(pieces, coupling[0], width_ref, mixed_ref), axis=1)
    lines = [ends_of(answers[side]) for side in range(2)]
    for edge in range(2):
        for side in range(2):
            own = value[edge * 2 + side : edge * 2 + side + 1]
            late[edge * 2 + side : edge * 2 + side + 1] = with_edges(
                edge, lines[side][edge : edge + 1], value[side : side + 1], own
            )
    for k in range(1, slabs):
        last_link(k).start()
    late_in[slab, 0:4] = late[0:4]
    for k in range(1, slabs):
        last_link(k).wait()
    carry_in, carry_next = chain(
        lambda d: late_in[d, 0:2], lambda d: late_in[d, 2:4], value[0:2]
    )
    for side in range(2):
        face_ref[side] = answers[side] + spread(
            carry_in[side : side + 1], carry_next[side : side + 1]
        )

    def wait_sent(c, unused):
        to_pair(c).wait_send()

        @pl.when(z < outer - 1)
        def _():
            to_above(c).wait_send()

        @pl.when(z > 0)
        def _():
            to_below(c).wait_send()

        return unused

    lax.fori_loop(0, chunks, wait_sent, 0)


def finish_kernel(parts, z_ref, face_ref, coef_ref, out_hbm, out_ref, sem):
    planes, width, depth = z_ref.shape
    rows = width // parts

    def store(c):
        at = pl.ds(pl.multiple_of(c * rows, 8), rows)
        return pltpu.make_async_copy(out_ref.at[:, at], out_hbm.at[:, at], sem.at[c])

    def part(c, unused):
        at = pl.ds(pl.multiple_of(c * rows, 8), rows)
        enter, leave = face_ref[0, at], face_ref[1, at]
        for j in range(planes):
            k = planes - 1 - j
            out_ref[j, at] = z_ref[j, at] + coef_ref[j : j + 1] * enter + coef_ref[k : k + 1] * leave
        store(c).start()
        return unused

    lax.fori_loop(0, parts, part, 0)

    def drain(c, unused):
        store(c).wait()
        return unused

    lax.fori_loop(0, parts, drain, 0)


def per_device(density, source, coupling, width_inverse, height_inverse, depth_inverse):
    planes, width, depth = density.shape
    pencils, slabs = lax.axis_size("pencil"), lax.axis_size("slab")
    blocks, size = width_inverse.shape[:2]
    group = 2
    half = width // 2
    extra = -(-2 * half // depth // 8) * 8
    seg = half + extra
    chunks = next(k for k in range(5, seg) if seg // 8 % k == 0)
    chunk = seg // chunks
    vmem = pl.BlockSpec(memory_space=pltpu.VMEM)
    hbm = pl.BlockSpec(memory_space=pl.ANY)
    smem = pl.BlockSpec(memory_space=pltpu.SMEM)
    dma = pltpu.SemaphoreType.DMA
    field = jax.ShapeDtypeStruct((planes, width, depth), F32)
    faces = jax.ShapeDtypeStruct((2, width, depth), F32)
    table = jax.ShapeDtypeStruct((planes, depth), F32)
    line = pltpu.VMEM((seg, depth), F32)
    two = pltpu.VMEM((2, seg, depth), F32)
    steps = dma((chunks,))
    peers = dma((slabs - 1,))
    z, face, table = pl.pallas_call(
        lambda *refs: step_kernel(group, pencils, slabs, chunk, *refs),
        out_shape=(field, faces, table),
        in_specs=[smem, hbm, hbm, vmem, vmem],
        out_specs=(vmem, vmem, vmem),
        scratch_shapes=[
            pltpu.VMEM((planes, width + 16, depth), F32),
            pltpu.VMEM((planes, width, depth), F32),
            pltpu.VMEM((planes, 2 * seg, depth), F32),
            pltpu.VMEM((blocks, 2 * size, 2 * size), BF16),
            pltpu.VMEM((2 * size, 2 * size), BF16),
            two, two, two, line, line, line, line, two,
            pltpu.VMEM((2, 2 * seg, depth), F32),
            pltpu.VMEM((2, planes, width), F32),
            pltpu.VMEM((slabs, 2, planes, width), F32),
            pltpu.VMEM((2, planes, width), F32),
            pltpu.VMEM((8, width), F32),
            pltpu.VMEM((slabs, 8, width), F32),
            dma((4 + 4 * (half // depth),)),
            steps, steps, steps, steps, steps, steps, steps, steps,
            peers, peers, peers, peers,
        ],
        compiler_params=pltpu.CompilerParams(
            vmem_limit_bytes=44 * 1024 * 1024, collective_id=0, has_side_effects=True
        ),
    )(coupling, density, source, width_inverse, depth_inverse)

    parts = 8
    return pl.pallas_call(
        lambda *refs: finish_kernel(parts, *refs),
        out_shape=field,
        in_specs=[vmem, vmem, vmem],
        out_specs=hbm,
        scratch_shapes=[pltpu.VMEM((planes, width, depth), F32), dma((parts,))],
        compiler_params=pltpu.CompilerParams(vmem_limit_bytes=32 * 1024 * 1024),
    )(z, face, table)


def solution(mesh):
    in_specs = (P("pencil", None, "slab"), P("pencil", None, "slab"), P(), P(), P(), P())
    out_specs = P("pencil", None, "slab")
    return jax.shard_map(
        per_device, mesh=mesh, in_specs=in_specs, out_specs=out_specs, check_vma=False
    )
```

time: 85.7 us -> 57.1 us (0.67)
  the two profiles are of different devices: /device:TPU:31 before, /device:TPU:0 now
where the time goes in v1:
time: 57.1 us; the launch traced here: 56.9 us
  Pallas kernels  54.3 us (95%)
  local copies, waits for them, and re-layouts  2.6 us (5%)
    pallas_call x1, Pallas kernels, per_device(): pl.pallas_call(lambda *refs: step_kernel(group, pencils, slabs, chunk, *r...  51.5 us
    pallas_call x1, Pallas kernels, per_device(): pl.pallas_call(lambda *refs: finish_kernel(parts, *refs), out_shape=field...  2.84 us
    unnamed x6, local copies, waits for them, and re-layouts  2.6 us

profile of v1, /device:TPU:0, one launch (start us, length us, event | category | flops | bytes accessed | tf_op | source)
XLA Modules:
  0.0 56.9 jit_solution(18143655561133549145)
XLA Ops:
  0.0 0.0 copy-start
  0.0 1.0 %copy-done = f32[6,128,128]{2,1,0:T(8,128)S(1)} copy-done((f32[6,128,128]{2,1,0:T(8,128)S(1)}, f32[6,128,128]{2,1,0:T(8,128)}, u32[]{:S(2)}) %copy-start) | copy-done | bytes 393240
  1.0 0.0 copy-start.1
  1.0 0.9 %copy-done.1 = f32[4,128,128]{2,1,0:T(8,128)S(1)} copy-done((f32[4,128,128]{2,1,0:T(8,128)S(1)}, f32[4,128,128]{2,1,0:T(8,128)}, u32[]{:S(2)}) %copy-start.1) | copy-done | bytes 262168
  1.9 0.0 copy-start.2
  1.9 0.7 %copy-done.2 = f32[3]{0:T(128)S(1)} copy-done((f32[3]{0:T(128)S(1)}, f32[3]{0:T(128)}, u32[]{:S(2)}) %copy-start.2) | copy-done | bytes 36
  2.6 51.5 %shard_map.55 = (f32[16,768,128]{2,1,0:T(8,128)S(1)}, f32[2,768,128]{2,1,0:T(8,128)S(1)}, f32[16,128]{1,0:T(8,128)S(1)}) custom-call(f32[3]{0:T(128)S(1)} %copy-done.2, f32[16,768,128]{2,1,0:T(8,128)} %refs_1_.1, f32[16,768,128]{2,1,0:T(8,128)} %refs_2_.1, f32[6,128,128]{2,1,0:T(8,128)S(1)} %copy-done, f32[4,128,128]{2,1,0:T(8,128)S(1)} %copy-done.1), custom_call_target="tpu_custom_call" | custom-call | tf_op jit(solution)/shard_map/pallas_call | solution.py:662
  54.1 2.8 %shard_map.56 = f32[16,768,128]{2,1,0:T(8,128)} custom-call(f32[16,768,128]{2,1,0:T(8,128)S(1)} %get-tuple-element.8.refs_0_, f32[2,768,128]{2,1,0:T(8,128)S(1)} %get-tuple-element.9.refs_1_, f32[16,128]{1,0:T(8,128)S(1)} %get-tuple-element.10.refs_2_), custom_call_target="tpu_custom_call" | custom-call | tf_op jit(solution)/shard_map/pallas_call | solution.py:690
Async XLA Ops:
  0.0 1.0 %copy-start = (f32[6,128,128]{2,1,0:T(8,128)S(1)}, f32[6,128,128]{2,1,0:T(8,128)}, u32[]{:S(2)}) copy-start(f32[6,128,128]{2,1,0:T(8,128)} %refs_3_.1) | copy-start | bytes 1179652
  1.0 0.9 %copy-start.1 = (f32[4,128,128]{2,1,0:T(8,128)S(1)}, f32[4,128,128]{2,1,0:T(8,128)}, u32[]{:S(2)}) copy-start(f32[4,128,128]{2,1,0:T(8,128)} %refs_4_.1) | copy-start | bytes 786436
  1.9 0.7 %copy-start.2 = (f32[3]{0:T(128)S(1)}, f32[3]{0:T(128)}, u32[]{:S(2)}) copy-start(f32[3]{0:T(128)} %refs_0_.1) | copy-start | bytes 40

commit v2 on v1

--- a/solution.py
+++ b/solution.py
@@ -95,6 +95,15 @@
         return self.power(j + 1) * self.tail(count - j) / self.tail(count + 1)
 
 
+def named(label):
+    def wrap(function):
+        def inner(*args):
+            with jax.named_scope(label):
+                return function(*args)
+        return inner
+    return wrap
+
+
 def rows_solve(pieces, strength, width_ref, mixed_ref):
     count, size = width_ref.shape[:2]
     local = []
@@ -118,14 +127,15 @@
 
 
 def step_kernel(
-    group, pencils, slabs, chunk,
-    coupling,
-    rho_hbm, source_hbm, width_ref, depth_ref,
+    group, pencils, slabs, chunk, lag,
+    coupling_hbm, rho_hbm, source_hbm, width_hbm, depth_hbm,
     z_ref, face_ref, coef_ref,
+    coupling, width_ref, depth_ref,
     rho_ref, source_ref, y_ref, mixed_ref, mixed_depth,
+    rho_edges, z_edges, turned, columns,
     pair_out, pair_in, block, up_out, up_in, down_out, down_in, back_out, final,
     ends, gathered, carries, late, late_in,
-    load_sem, pair_send, pair_recv, up_send, up_recv, down_send, down_recv,
+    load_sem, table_sem, pair_send, pair_recv, up_send, up_recv, down_send, down_recv,
     back_send, back_recv, early_send, early_recv, late_send, late_recv,
 ):
     planes, width, depth = z_ref.shape
@@ -175,6 +185,13 @@
         start = h * half + piece * depth
         return load(("source", turn, piece), source_hbm, source_ref, start, depth, 0)
 
+    tables = [
+        pltpu.make_async_copy(src, dst, table_sem.at[k])
+        for k, (src, dst) in enumerate(
+            ((coupling_hbm, coupling), (width_hbm, width_ref), (depth_hbm, depth_ref))
+        )
+    ]
+    tables[0].start()
     for h in (0, 1):
         for side in (0, 1):
             rim(h, side).start()
@@ -182,21 +199,13 @@
         for piece in range(strips):
             main(turn, h, piece).start()
             other(turn, h, piece).start()
+        if turn == 0:
+            tables[1].start()
+            tables[2].start()
 
     rho_ref[:, :pad] = jnp.zeros((planes, pad, depth), F32)
     rho_ref[:, pad + width :] = jnp.zeros((planes, pad, depth), F32)
-    for i in range(count):
-        high, low = split(width_ref[i])
-        mixed_ref[i, :size, :size] = high
-        mixed_ref[i, :size, size:] = high
-        mixed_ref[i, size:, :size] = low
-        mixed_ref[i, size:, size:] = jnp.zeros_like(low)
-    high, low = split(depth_ref[slab])
-    mixed_depth[:size, :size] = high
-    mixed_depth[size:, :size] = high
-    mixed_depth[:size, size:] = low
-    mixed_depth[size:, size:] = jnp.zeros_like(low)
-
+    tables[0].wait()
     heights = Heights(coupling[1], depth)
     for j in range(planes):
         coef_ref[j : j + 1] = heights.enter(planes, j)
@@ -228,11 +237,13 @@
             y_ref[j, at] = y
         return y
 
+    @named("sweep")
     def sweep(h, row, rows):
         base = pl.multiple_of(pad + h * half + row, 8)
         at = pl.ds(pl.multiple_of(h * seg + row, 8), rows)
         from_source = pl.ds(pl.multiple_of(h * half + row, 8), rows)
         value = None
+        edges = jnp.zeros((rows, depth), F32)
         for j in range(planes):
             rho = rho_ref[j, pl.ds(base, rows)]
             beside = rho_ref[j, pl.ds(base - 1, rows)] + rho_ref[j, pl.ds(base + 1, rows)]
@@ -243,30 +254,26 @@
                 + k_before * pltpu.roll(rho, 1, 1)
                 + k_after * pltpu.roll(rho, depth - 1, 1)
             )
+            edges = jnp.where(lax.div(lane, 2) == j, pltpu.roll(rho, 2 * j + 1, 1), edges)
             value = rhs if j == 0 else rhs + ahead[j - 1] * value
             y_ref[j, at] = value
+        rho_edges[from_source] = edges
         last = pivot[planes - 1] * value
         first = back_sweep(at, value)
         return first, last
 
+    @named("edge")
     def edge_sweep(h):
         at = pl.ds(pl.multiple_of(h * seg + half, 8), extra)
         value = None
-        row = lax.broadcasted_iota(jnp.int32, (depth, depth), 0)
-        column = lax.broadcasted_iota(jnp.int32, (depth, depth), 1)
-
-        def gather(j, unused):
-            lines = []
-            for edge in (0, depth - 1):
-                for strip in range(strips):
-                    start = pl.multiple_of(pad + h * half + strip * depth, 8)
-                    piece = rho_ref[j, pl.ds(start, depth)][:, edge : edge + 1]
-                    lines.append(jnp.sum(jnp.where(row == column, piece, 0.0), axis=0, keepdims=True))
-            lines.append(jnp.zeros((extra - 2 * strips, depth), F32))
-            y_ref[j, at] = jnp.concatenate(lines, axis=0)
-            return unused
-
-        lax.fori_loop(0, planes, gather, 0)
+        for strip in range(strips):
+            start = pl.multiple_of(h * half + strip * depth, 8)
+            rows = rho_edges[pl.ds(start, depth)].T
+            for j in range(planes):
+                to = pl.ds(h * seg + half + 2 * strip, 2)
+                y_ref[j, to] = rows[2 * j : 2 * j + 2]
+        spare = extra - 2 * strips
+        y_ref[:, pl.ds(h * seg + half + 2 * strips, spare)] = jnp.zeros((planes, spare, depth), F32)
         for j in range(planes):
             rhs = y_ref[j, at]
             value = rhs if j == 0 else rhs + ahead[j - 1] * value
@@ -306,34 +313,63 @@
             back_send.at[c], back_recv.at[c], pair,
         )
 
-    for turn, h in ((0, 1 - x), (1, x)):
+    def keep(turn, at, faces):
         if turn == 0:
-            for hh in (0, 1):
-                for side in (0, 1):
-                    rim(hh, side).wait()
-        ready = 0
-        for c in range(chunks):
-            need = min(strips, -(-(c * chunk + chunk + 1) // depth))
-            while ready < need:
-                main(turn, h, ready).wait()
-                other(turn, h, ready).wait()
-                ready += 1
-            row = c * chunk
-            at = pl.ds(row, min(chunk, half - row))
-            first, last = sweep(h, row, min(chunk, half - row))
-            if turn == 0:
-                pair_out[0, at] = first
-                pair_out[1, at] = last
-            if c == chunks - 1:
-                at = pl.ds(half, extra)
-                first, last = edge_sweep(h)
-                if turn == 0:
-                    pair_out[0, at] = first
-                    pair_out[1, at] = last
-            if turn == 0:
-                if c == 0:
-                    pl.semaphore_wait(barrier, 3 + slabs - 1)
-                to_pair(c).start()
+            pair_out[0, at], pair_out[1, at] = faces
+
+    need = [min(strips, -(-(c * chunk + chunk + 1) // depth)) for c in range(chunks)]
+    first_use = [next(c for c in range(chunks) if need[c] > piece) for piece in range(strips)]
+
+    def whole_chunk(turn, h, c):
+        for piece in range(strips):
+            @pl.when(c == first_use[piece])
+            def _():
+                main(turn, h, piece).wait()
+                other(turn, h, piece).wait()
+
+        row = pl.multiple_of(c * chunk, 8)
+        keep(turn, pl.ds(row, chunk), sweep(h, row, chunk))
+
+    def last_chunk(turn, h):
+        for piece in range(strips):
+            if first_use[piece] == chunks - 1:
+                main(turn, h, piece).wait()
+                other(turn, h, piece).wait()
+        row = (chunks - 1) * chunk
+        keep(turn, pl.ds(row, half - row), sweep(h, row, half - row))
+        keep(turn, pl.ds(half, extra), edge_sweep(h))
+
+    for h in (0, 1):
+        for side in (0, 1):
+            rim(h, side).wait()
+
+    def for_pair(c, unused):
+        whole_chunk(0, 1 - x, c)
+
+        @pl.when(c == 0)
+        def _():
+            pl.semaphore_wait(barrier, 3 + slabs - 1)
+
+        to_pair(c).start()
+        return unused
+
+    lax.fori_loop(0, chunks - 1, for_pair, 0)
+    last_chunk(0, 1 - x)
+    to_pair(chunks - 1).start()
+    tables[1].wait()
+    tables[2].wait()
+    for i in range(count):
+        high, low = split(width_ref[i])
+        mixed_ref[i, :size, :size] = high
+        mixed_ref[i, :size, size:] = high
+        mixed_ref[i, size:, :size] = low
+        mixed_ref[i, size:, size:] = jnp.zeros_like(low)
+    high, low = split(depth_ref[slab])
+    mixed_depth[:size, :size] = high
+    mixed_depth[size:, :size] = high
+    mixed_depth[:size, size:] = low
+    mixed_depth[size:, size:] = jnp.zeros_like(low)
+
 
     @pl.when(z == 0)
     def _():
@@ -355,6 +391,7 @@
             jnp.where(lower, its_last, own_last),
         )
 
+    @named("pair")
     def do_pair(c):
         to_pair(c).wait_recv()
         at = rows_at(c)
@@ -362,6 +399,7 @@
         block[0, at] = f0 + far * gain * (f1 + near * l0)
         block[1, at] = l1 + far * gain * (l0 + near * f1)
 
+    @named("up")
     def do_up(c):
         @pl.when(z > 0)
         def _():
@@ -374,6 +412,7 @@
             up_out[at] = block[1, at] + far2 * under_gain * (up_in[at] + under * block[0, at])
             to_above(c).start()
 
+    @named("down")
     def do_down(c):
         @pl.when(z < outer - 1)
         def _():
@@ -386,6 +425,7 @@
             down_out[at] = block[0, at] + far2 * over_gain * (down_in[at] + over * block[1, at])
             to_below(c).start()
 
+    @named("done")
     def do_final(c):
         at, mine = rows_at(c), rows_at(c, x * seg)
         low = up_in[at] + under * block[0, at]
@@ -407,6 +447,7 @@
     def blocks_at(i):
         return pl.ds(i // strips * seg + i % strips * size, size)
 
+    @named("mid")
     def solve_planes(index):
         base = index * group
         rhs = jnp.concatenate(
@@ -426,9 +467,12 @@
         answers = solve_group(rhs, coupling[0], width_ref, mixed_ref, mixed_depth[...])
         for g in range(group):
             z_ref[base + g] = answers[g] + rho_ref[base + g, pl.ds(pad, width)]
-            lines = ends_of(answers[g])
-            ends[0, pl.ds(base + g, 1)] = lines[0:1]
-            ends[1, pl.ds(base + g, 1)] = lines[1:2]
+            rolled = pltpu.roll(answers[g], 2 * (base + g) + 1, 1)
+            z_edges[...] = jnp.where(lax.div(lane, 2) == base + g, rolled, z_edges[...])
+
+    def turn_rows(source, i, rows):
+        turned[i] = source[pl.ds(i * size, size)].T[: turned.shape[1]]
+        return [turned[i, pl.ds(edge, rows, stride=2)] for edge in (1, 0)]
 
     before_me = jnp.where(slab > 0, slab - 1, 0)
     corner = depth_ref[before_me, size - 1 : size, size - 1 : size]
@@ -441,19 +485,22 @@
         row = 0 if edge == 0 else size - 1
         return ends_value + 2.0 * v_own + (2.0 * coupling[2] * corner * link(slab, row, 0)) * v_first
 
+    @named("early")
     def early_edges():
         pieces = []
         for i in range(count):
             h, strip = i // strips, i % strips
             rows = [
-                y_ref[:, h * seg + half + edge * strips + strip, :] for edge in (0, 1)
+                y_ref[:, h * seg + half + 2 * strip + 1 - edge, :] for edge in (0, 1)
             ]
             pieces.append(jnp.concatenate(rows, axis=0))
         value = jnp.concatenate(rows_solve(pieces, coupling[0], width_ref, mixed_ref), axis=1)
         first, last = value[:planes], value[planes:]
         carries[0] = first
-        ends[0] = with_edges(0, ends[0], first, first)
-        ends[1] = with_edges(1, ends[1], first, last)
+        lines = [turn_rows(z_edges, i, planes) for i in range(count)]
+        lines = [jnp.concatenate([line[edge] for line in lines], axis=1) for edge in (0, 1)]
+        ends[0] = with_edges(0, lines[0], first, first)
+        ends[1] = with_edges(1, lines[1], first, last)
         for k in range(1, slabs):
             early(k).start()
         gathered[slab] = ends[...]
@@ -487,51 +534,50 @@
             carry_next = jnp.where(slab == d, backward[d], carry_next)
         return carry_in + (2.0 * coupling[2] * corner) * v_first, carry_next
 
-    def spread(carry_in, carry_next):
-        in_high, in_low = split(coupling[2] * depth_ref[slab, 0:1])
-        next_high, next_low = split(coupling[2] * depth_ref[slab, size - 1 : size])
-        rhs = rows_of((in_high, in_high, in_low, next_high, next_high, next_low), depth)
-        a_high, a_low = split(carry_in)
-        b_high, b_low = split(carry_next)
-        lhs = rows_of((a_high, a_low, a_high, b_high, b_low, b_high), width)
-        return dot(lhs, rhs, ((0,), (0,)))
-
-    per_tick = 2
-    busy = -(-groups // per_tick)
-    ticks = max(chunks + outer - 1, busy + 1)
+    reach = lag * (outer - 1)
+    ticks = max(chunks + reach, groups + 2)
+    ready = (chunks + 1) // 2
 
     def tick(t, unused):
+        @pl.when(t < 2)
+        def _():
+            def ours(c, same):
+                whole_chunk(1, x, c)
+                return same
+
+            lax.fori_loop(t * ready, jnp.minimum(t * ready + ready, chunks - 1), ours, 0)
+
+        @pl.when(t == 1)
+        def _():
+            last_chunk(1, x)
+
         @pl.when(t < chunks)
         def _():
             do_pair(t)
 
-        up = t - z
+        up = t - lag * z
 
         @pl.when((up >= 0) & (up < chunks))
         def _():
             do_up(up)
 
-        down = t - (outer - 1 - z)
+        down = t - lag * (outer - 1 - z)
 
         @pl.when((down >= 0) & (down < chunks))
         def _():
             do_down(down)
 
-        done = t - jnp.maximum(z, outer - 1 - z)
+        done = t - lag * jnp.maximum(z, outer - 1 - z)
 
         @pl.when((done >= 0) & (done < chunks))
         def _():
             do_final(done)
 
-        @pl.when(t < busy)
-        def _():
-            def one(k, same):
-                solve_planes(t * per_tick + k)
-                return same
-
-            lax.fori_loop(0, per_tick, one, 0)
-
-        @pl.when(t == busy)
+        @pl.when((t >= 1) & (t <= groups))
+        def _():
+            solve_planes(t - 1)
+
+        @pl.when(t == groups + 1)
         def _():
             early_edges()
 
@@ -539,63 +585,98 @@
 
     lax.fori_loop(0, ticks, tick, 0)
 
+    @named("back")
+    def wait_back(c, unused):
+        to_back(c).wait()
+        return unused
+
+    lax.fori_loop(0, chunks, wait_back, 0)
+    with jax.named_scope("late_solve"):
+        rhs = jnp.concatenate(
+            [
+                jnp.concatenate([final[side, blocks_at(i)] for i in range(count)], axis=0)
+                for side in range(2)
+            ],
+            axis=1,
+        )
+        answers = solve_group(rhs, coupling[0], width_ref, mixed_ref, mixed_depth[...])
+        pieces = []
+        for i in range(count):
+            h, strip = i // strips, i % strips
+            rows = [
+                final[side, h * seg + half + 2 * strip + 1 - edge, :].reshape(1, depth)
+                for edge in (0, 1) for side in (0, 1)
+            ]
+            rows.append(jnp.zeros((4, depth), F32))
+            pieces.append(jnp.concatenate(rows, axis=0))
+        value = jnp.concatenate(rows_solve(pieces, coupling[0], width_ref, mixed_ref), axis=1)
+        edges = jnp.where(lax.div(lane, 2) == 0, pltpu.roll(answers[0], 1, 1), pltpu.roll(answers[1], 3, 1))
+        z_edges[...] = edges
+        lines = [turn_rows(z_edges, i, 2) for i in range(count)]
+        lines = [jnp.concatenate([line[edge] for line in lines], axis=1) for edge in (0, 1)]
+        for edge in range(2):
+            for side in range(2):
+                own = value[edge * 2 + side : edge * 2 + side + 1]
+                late[edge * 2 + side : edge * 2 + side + 1] = with_edges(
+                    edge, lines[edge][side : side + 1], value[side : side + 1], own
+                )
     for k in range(1, slabs):
-        early(k).wait()
+        last_link(k).start()
+    late_in[slab, 0:4] = late[0:4]
+
+    with jax.named_scope("early_wait"):
+        for k in range(1, slabs):
+            early(k).wait()
+    in_row = coupling[2] * depth_ref[slab, 0:1]
+    next_row = coupling[2] * depth_ref[slab, size - 1 : size]
+    (in_high, in_low), (next_high, next_low) = split(in_row), split(next_row)
+    spots = lax.broadcasted_iota(jnp.int32, (2 * depth, depth), 0)
+    number, spot = lax.div(spots, planes), lax.rem(spots, planes)
+    lows = depth // planes
+    base = jnp.zeros((2 * depth, depth), F32)
+    for k, piece in (
+        (0, in_high), (1, next_high), (2, in_low), (3, next_low),
+        (lows, in_high), (lows + 1, next_high),
+    ):
+        base = jnp.where(number == k, piece.astype(F32), base)
     carry_in, carry_next = chain(
         lambda d: gathered[d, 0], lambda d: gathered[d, 1], carries[0]
     )
-    carries[0] = carry_in
-    carries[1] = carry_next
-
-    def finish_plane(j, unused):
-        z_ref[j] = z_ref[j] + spread(carries[0, pl.ds(j, 1)], carries[1, pl.ds(j, 1)])
+    lines = jnp.concatenate([carry_in, carry_next] * 2, axis=0)
+    lines = jnp.concatenate([lines, jnp.zeros((depth - 4 * planes, width), F32)], axis=0)
+    for i in range(count):
+        part = slice(i * size, (i + 1) * size)
+        columns[part] = both(lines[:, part].T, 1)
+
+    @named("fix")
+    def finish_planes(index, unused):
+        j = index * group
+        rhs = jnp.concatenate([jnp.where(spot == j + g, base, 0.0) for g in range(group)], axis=1)
+        both_planes = dot(columns[...], rhs.astype(BF16), ((1,), (0,)))
+        for g in range(group):
+            z_ref[j + g] = z_ref[j + g] + both_planes[:, g * depth : (g + 1) * depth]
         return unused
 
-    lax.fori_loop(0, planes, finish_plane, 0)
-
-    def wait_back(c, unused):
-        to_back(c).wait()
-        return unused
-
-    lax.fori_loop(0, chunks, wait_back, 0)
-    rhs = jnp.concatenate(
-        [
-            jnp.concatenate([final[side, blocks_at(i)] for i in range(count)], axis=0)
-            for side in range(2)
-        ],
-        axis=1,
-    )
-    answers = solve_group(rhs, coupling[0], width_ref, mixed_ref, mixed_depth[...])
-    pieces = []
-    for i in range(count):
-        h, strip = i // strips, i % strips
-        rows = [
-            final[side, h * seg + half + edge * strips + strip, :].reshape(1, depth)
-            for edge in (0, 1) for side in (0, 1)
-        ]
-        rows.append(jnp.zeros((4, depth), F32))
-        pieces.append(jnp.concatenate(rows, axis=0))
-    value = jnp.concatenate(rows_solve(pieces, coupling[0], width_ref, mixed_ref), axis=1)
-    lines = [ends_of(answers[side]) for side in range(2)]
-    for edge in range(2):
-        for side in range(2):
-            own = value[edge * 2 + side : edge * 2 + side + 1]
-            late[edge * 2 + side : edge * 2 + side + 1] = with_edges(
-                edge, lines[side][edge : edge + 1], value[side : side + 1], own
-            )
-    for k in range(1, slabs):
-        last_link(k).start()
-    late_in[slab, 0:4] = late[0:4]
-    for k in range(1, slabs):
-        last_link(k).wait()
+    lax.fori_loop(0, groups, finish_planes, 0)
+    with jax.named_scope("late_wait"):
+        for k in range(1, slabs):
+            last_link(k).wait()
     carry_in, carry_next = chain(
         lambda d: late_in[d, 0:2], lambda d: late_in[d, 2:4], value[0:2]
     )
+    pieces = []
     for side in range(2):
-        face_ref[side] = answers[side] + spread(
-            carry_in[side : side + 1], carry_next[side : side + 1]
-        )
-
+        (a_high, a_low), (b_high, b_low) = split(carry_in[side : side + 1]), split(carry_next[side : side + 1])
+        pieces += [a_high, a_low, a_high, b_high, b_low, b_high]
+    six = (in_high, in_high, in_low, next_high, next_high, next_low)
+    blank = jnp.zeros((1, depth), F32)
+    row_pairs = [jnp.concatenate([piece.astype(F32), blank], axis=1) for piece in six]
+    row_pairs += [jnp.concatenate([blank, piece.astype(F32)], axis=1) for piece in six]
+    spread = dot(rows_of(pieces, width), rows_of(row_pairs, 2 * depth), ((0,), (0,)))
+    for side in range(2):
+        face_ref[side] = answers[side] + spread[:, side * depth : (side + 1) * depth]
+
+    @named("sent")
     def wait_sent(c, unused):
         to_pair(c).wait_send()
 
@@ -650,7 +731,7 @@
     chunk = seg // chunks
     vmem = pl.BlockSpec(memory_space=pltpu.VMEM)
     hbm = pl.BlockSpec(memory_space=pl.ANY)
-    smem = pl.BlockSpec(memory_space=pltpu.SMEM)
+    far = pl.BlockSpec(memory_space=pltpu.HBM)
     dma = pltpu.SemaphoreType.DMA
     field = jax.ShapeDtypeStruct((planes, width, depth), F32)
     faces = jax.ShapeDtypeStruct((2, width, depth), F32)
@@ -660,16 +741,23 @@
     steps = dma((chunks,))
     peers = dma((slabs - 1,))
     z, face, table = pl.pallas_call(
-        lambda *refs: step_kernel(group, pencils, slabs, chunk, *refs),
+        lambda *refs: step_kernel(group, pencils, slabs, chunk, 2, *refs),
         out_shape=(field, faces, table),
-        in_specs=[smem, hbm, hbm, vmem, vmem],
+        in_specs=[far, far, far, far, far],
         out_specs=(vmem, vmem, vmem),
         scratch_shapes=[
+            pltpu.SMEM(coupling.shape, F32),
+            pltpu.VMEM(width_inverse.shape, F32),
+            pltpu.VMEM(depth_inverse.shape, F32),
             pltpu.VMEM((planes, width + 16, depth), F32),
             pltpu.VMEM((planes, width, depth), F32),
             pltpu.VMEM((planes, 2 * seg, depth), F32),
             pltpu.VMEM((blocks, 2 * size, 2 * size), BF16),
             pltpu.VMEM((2 * size, 2 * size), BF16),
+            pltpu.VMEM((width, depth), F32),
+            pltpu.VMEM((width, depth), F32),
+            pltpu.VMEM((blocks, 2 * planes, depth), F32),
+            pltpu.VMEM((width, 2 * depth), BF16),
             two, two, two, line, line, line, line, two,
             pltpu.VMEM((2, 2 * seg, depth), F32),
             pltpu.VMEM((2, planes, width), F32),
@@ -677,7 +765,7 @@
             pltpu.VMEM((2, planes, width), F32),
             pltpu.VMEM((8, width), F32),
             pltpu.VMEM((slabs, 8, width), F32),
-            dma((4 + 4 * (half // depth),)),
+            dma((4 + 4 * (half // depth),)), dma((3,)),
             steps, steps, steps, steps, steps, steps, steps, steps,
             peers, peers, peers, peers,
         ],

time: 57.1 us -> 42.7 us (0.75)
  Pallas kernels: 54.3 us -> 39.9 us
    pallas_call x1, Pallas kernels: 51.5 us -> 37 us  [per_device(): pl.pallas_call(lambda *refs: step_kernel(group, pencils, slabs, chunk, 2,...]
where the time goes in v2:
time: 42.7 us; the launch traced here: 42.5 us
  Pallas kernels  39.9 us (93%)
  local copies, waits for them, and re-layouts  2.6 us (6%)
    pallas_call x1, Pallas kernels, per_device(): pl.pallas_call(lambda *refs: step_kernel(group, pencils, slabs, chunk, 2,...  37 us
    pallas_call x1, Pallas kernels, per_device(): pl.pallas_call(lambda *refs: finish_kernel(parts, *refs), out_shape=field...  2.84 us
    unnamed x6, local copies, waits for them, and re-layouts  2.6 us

profile of v2, /device:TPU:0, one launch (start us, length us, event | category | flops | bytes accessed | tf_op | source)
XLA Modules:
  0.0 42.5 jit_solution(1953104083116243008)
XLA Ops:
  0.0 0.0 copy-start
  0.0 1.0 %copy-done = f32[6,128,128]{2,1,0:T(8,128)S(1)} copy-done((f32[6,128,128]{2,1,0:T(8,128)S(1)}, f32[6,128,128]{2,1,0:T(8,128)}, u32[]{:S(2)}) %copy-start) | copy-done | bytes 393240
  1.0 0.0 copy-start.1
  1.0 0.9 %copy-done.1 = f32[4,128,128]{2,1,0:T(8,128)S(1)} copy-done((f32[4,128,128]{2,1,0:T(8,128)S(1)}, f32[4,128,128]{2,1,0:T(8,128)}, u32[]{:S(2)}) %copy-start.1) | copy-done | bytes 262168
  1.9 0.0 copy-start.2
  1.9 0.7 %copy-done.2 = f32[3]{0:T(128)S(1)} copy-done((f32[3]{0:T(128)S(1)}, f32[3]{0:T(128)}, u32[]{:S(2)}) %copy-start.2) | copy-done | bytes 36
  2.6 37.0 %shard_map.55 = (f32[16,768,128]{2,1,0:T(8,128)S(1)}, f32[2,768,128]{2,1,0:T(8,128)S(1)}, f32[16,128]{1,0:T(8,128)S(1)}) custom-call(f32[3]{0:T(128)S(1)} %copy-done.2, f32[16,768,128]{2,1,0:T(8,128)} %refs_1_.1, f32[16,768,128]{2,1,0:T(8,128)} %refs_2_.1, f32[6,128,128]{2,1,0:T(8,128)S(1)} %copy-done, f32[4,128,128]{2,1,0:T(8,128)S(1)} %copy-done.1), custom_call_target="tpu_custom_call" | custom-call | tf_op jit(solution)/shard_map/pallas_call | solution.py:743
  39.6 2.8 %shard_map.56 = f32[16,768,128]{2,1,0:T(8,128)} custom-call(f32[16,768,128]{2,1,0:T(8,128)S(1)} %get-tuple-element.8.refs_0_, f32[2,768,128]{2,1,0:T(8,128)S(1)} %get-tuple-element.9.refs_1_, f32[16,128]{1,0:T(8,128)S(1)} %get-tuple-element.10.refs_2_), custom_call_target="tpu_custom_call" | custom-call | tf_op jit(solution)/shard_map/pallas_call | solution.py:778
Async XLA Ops:
  0.0 1.0 %copy-start = (f32[6,128,128]{2,1,0:T(8,128)S(1)}, f32[6,128,128]{2,1,0:T(8,128)}, u32[]{:S(2)}) copy-start(f32[6,128,128]{2,1,0:T(8,128)} %refs_3_.1) | copy-start | bytes 1179652
  1.0 0.9 %copy-start.1 = (f32[4,128,128]{2,1,0:T(8,128)S(1)}, f32[4,128,128]{2,1,0:T(8,128)}, u32[]{:S(2)}) copy-start(f32[4,128,128]{2,1,0:T(8,128)} %refs_4_.1) | copy-start | bytes 786436
  1.9 0.7 %copy-start.2 = (f32[3]{0:T(128)S(1)}, f32[3]{0:T(128)}, u32[]{:S(2)}) copy-start(f32[3]{0:T(128)} %refs_0_.1) | copy-start | bytes 40

commit v3 on v2

--- a/solution.py
+++ b/solution.py
@@ -44,9 +44,8 @@
     return value.astype(BF16)
 
 
-def solve_group(rhs, strength, width_ref, mixed_ref, depth_mixed):
+def width_solve(rhs, strength, width_ref, mixed_ref):
     count, size = width_ref.shape[:2]
-    depth = size
     total = rhs.shape[1]
     high, low = split(rhs)
     local, starts, stops = [], [], []
@@ -67,12 +66,13 @@
     for i in reversed(range(count)):
         solved[i] = local[i] + starts[i] * ahead[i] + stops[i] * carry
         carry = heads[i] + stops[i][0:1] * carry
-    solved = jnp.concatenate(solved, axis=0)
-    answers = []
-    for start in range(0, total, depth):
-        product = dot(both(solved[:, start : start + depth], 1), depth_mixed, ((1,), (0,)))
-        answers.append(product[:, :depth] + product[:, depth:])
-    return answers
+    return jnp.concatenate(solved, axis=0)
+
+
+def depth_solve(value, mixed_depth):
+    depth = value.shape[1]
+    product = dot(both(value, 1), mixed_depth[...], ((1,), (0,)))
+    return product[:, :depth] + product[:, depth:]
 
 
 class Heights:
@@ -132,11 +132,11 @@
     z_ref, face_ref, coef_ref,
     coupling, width_ref, depth_ref,
     rho_ref, source_ref, y_ref, mixed_ref, mixed_depth,
-    rho_edges, z_edges, turned, columns,
+    shifts, at_ends, rho_edges, z_edges, turned, columns,
     pair_out, pair_in, block, up_out, up_in, down_out, down_in, back_out, final,
     ends, gathered, carries, late, late_in,
     load_sem, table_sem, pair_send, pair_recv, up_send, up_recv, down_send, down_recv,
-    back_send, back_recv, early_send, early_recv, late_send, late_recv,
+    back_send, back_recv, early_send, early_recv, own_send, own_recv, cross_send, cross_recv,
 ):
     planes, width, depth = z_ref.shape
     groups = planes // group
@@ -158,9 +158,9 @@
     for peer in (pair, above_me, below_me):
         pl.semaphore_signal(barrier, inc=1, device_id={"pencil": peer}, device_id_type=MESH)
     for k in range(1, slabs):
-        pl.semaphore_signal(
-            barrier, inc=1, device_id={"slab": lax.rem(slab + k, slabs)}, device_id_type=MESH
-        )
+        peer = lax.rem(slab + k, slabs)
+        for whom in ({"slab": peer}, {"pencil": pair, "slab": peer}):
+            pl.semaphore_signal(barrier, inc=1, device_id=whom, device_id_type=MESH)
 
     loads = {}
 
@@ -195,11 +195,11 @@
     for h in (0, 1):
         for side in (0, 1):
             rim(h, side).start()
-    for turn, h in ((0, 1 - x), (1, x)):
-        for piece in range(strips):
+    for piece in range(strips):
+        for turn, h in ((0, 1 - x), (1, x)):
             main(turn, h, piece).start()
             other(turn, h, piece).start()
-        if turn == 0:
+        if piece == 0:
             tables[1].start()
             tables[2].start()
 
@@ -225,8 +225,12 @@
     lane = lax.broadcasted_iota(jnp.int32, (1, depth), 1)
     across, along = coupling[0], coupling[2]
     k_here = 2.0 - 4.0 * across - 4.0 * along
-    k_before = jnp.where(lane == 0, 0.0, jnp.full((1, depth), 2.0 * along, F32))
-    k_after = jnp.where(lane == depth - 1, 0.0, jnp.full((1, depth), 2.0 * along, F32))
+    source_row = lax.rem(lax.broadcasted_iota(jnp.int32, (2 * depth, depth), 0), depth)
+    column = lax.broadcasted_iota(jnp.int32, (2 * depth, depth), 1)
+    beside_it = (source_row == column + 1) | (source_row == column - 1)
+    at_edge = source_row == jnp.where(lax.rem(column, 2) == 0, depth - 1, 0)
+    shifts[:, :depth] = jnp.where(beside_it, 1.0, 0.0).astype(BF16)
+    shifts[:, depth:] = jnp.where(at_edge, 1.0, 0.0).astype(BF16)
 
     def back_sweep(at, value):
         for j in reversed(range(planes)):
@@ -244,17 +248,22 @@
         from_source = pl.ds(pl.multiple_of(h * half + row, 8), rows)
         value = None
         edges = jnp.zeros((rows, depth), F32)
+        batch = 8
         for j in range(planes):
+            if j % batch == 0:
+                several = [rho_ref[j + k, pl.ds(base, rows)] for k in range(batch)]
+                several = both(jnp.concatenate(several, axis=0), 1)
+                all_shifted = dot(several, shifts[...], ((1,), (0,)))
             rho = rho_ref[j, pl.ds(base, rows)]
             beside = rho_ref[j, pl.ds(base - 1, rows)] + rho_ref[j, pl.ds(base + 1, rows)]
+            shifted = all_shifted[j % batch * rows : (j % batch + 1) * rows]
             rhs = (
                 source_ref[j, from_source]
                 + k_here * rho
                 + (2.0 * across) * beside
-                + k_before * pltpu.roll(rho, 1, 1)
-                + k_after * pltpu.roll(rho, depth - 1, 1)
+                + (2.0 * along) * shifted[:, :depth]
             )
-            edges = jnp.where(lax.div(lane, 2) == j, pltpu.roll(rho, 2 * j + 1, 1), edges)
+            edges = jnp.where(lax.div(lane, 2) == j, shifted[:, depth:], edges)
             value = rhs if j == 0 else rhs + ahead[j - 1] * value
             y_ref[j, at] = value
         rho_edges[from_source] = edges
@@ -282,10 +291,11 @@
         first = back_sweep(at, value)
         return first, last
 
-    def remote(source, target, send, recv, peer, axis="pencil"):
+    def remote(source, target, send, recv, peer):
+        whom = peer if isinstance(peer, dict) else {"pencil": peer}
         return pltpu.make_async_remote_copy(
             src_ref=source, dst_ref=target, send_sem=send, recv_sem=recv,
-            device_id={axis: peer}, device_id_type=MESH,
+            device_id=whom, device_id_type=MESH,
         )
 
     def rows_at(c, shift=0):
@@ -343,33 +353,33 @@
         for side in (0, 1):
             rim(h, side).wait()
 
-    def for_pair(c, unused):
-        whole_chunk(0, 1 - x, c)
-
-        @pl.when(c == 0)
-        def _():
-            pl.semaphore_wait(barrier, 3 + slabs - 1)
-
-        to_pair(c).start()
-        return unused
-
-    lax.fori_loop(0, chunks - 1, for_pair, 0)
-    last_chunk(0, 1 - x)
-    to_pair(chunks - 1).start()
-    tables[1].wait()
-    tables[2].wait()
-    for i in range(count):
-        high, low = split(width_ref[i])
-        mixed_ref[i, :size, :size] = high
-        mixed_ref[i, :size, size:] = high
-        mixed_ref[i, size:, :size] = low
-        mixed_ref[i, size:, size:] = jnp.zeros_like(low)
-    high, low = split(depth_ref[slab])
-    mixed_depth[:size, :size] = high
-    mixed_depth[size:, :size] = high
-    mixed_depth[:size, size:] = low
-    mixed_depth[size:, size:] = jnp.zeros_like(low)
-
+    def prepare():
+        tables[1].wait()
+        tables[2].wait()
+        for i in range(count):
+            high, low = split(width_ref[i])
+            mixed_ref[i, :size, :size] = high
+            mixed_ref[i, :size, size:] = high
+            mixed_ref[i, size:, :size] = low
+            mixed_ref[i, size:, size:] = jnp.zeros_like(low)
+        first_high, first_low = split(depth_ref[slab, 0:1])
+        last_high, last_low = split(depth_ref[slab, size - 1 : size])
+        nothing = jnp.zeros((1, depth), F32)
+        at_ends[...] = rows_of(
+            [
+                jnp.concatenate([piece.astype(F32), tail], axis=1)
+                for piece, tail in (
+                    (first_high, first_high.astype(F32)), (last_high, last_high.astype(F32)),
+                    (first_low, nothing), (last_low, nothing),
+                )
+            ],
+            2 * depth,
+        )
+        high, low = split(depth_ref[slab])
+        mixed_depth[:size, :size] = high
+        mixed_depth[size:, :size] = high
+        mixed_depth[:size, size:] = low
+        mixed_depth[size:, size:] = jnp.zeros_like(low)
 
     @pl.when(z == 0)
     def _():
@@ -464,7 +474,10 @@
             ],
             axis=1,
         )
-        answers = solve_group(rhs, coupling[0], width_ref, mixed_ref, mixed_depth[...])
+        solved = width_solve(rhs, coupling[0], width_ref, mixed_ref)
+        answers = [
+            depth_solve(solved[:, g * depth : (g + 1) * depth], mixed_depth) for g in range(group)
+        ]
         for g in range(group):
             z_ref[base + g] = answers[g] + rho_ref[base + g, pl.ds(pad, width)]
             rolled = pltpu.roll(answers[g], 2 * (base + g) + 1, 1)
@@ -474,16 +487,16 @@
         turned[i] = source[pl.ds(i * size, size)].T[: turned.shape[1]]
         return [turned[i, pl.ds(edge, rows, stride=2)] for edge in (1, 0)]
 
-    before_me = jnp.where(slab > 0, slab - 1, 0)
-    corner = depth_ref[before_me, size - 1 : size, size - 1 : size]
-    corner = jnp.where(slab > 0, corner, jnp.zeros_like(corner))
+    def corner():
+        value = depth_ref[jnp.where(slab > 0, slab - 1, 0), size - 1 : size, size - 1 : size]
+        return jnp.where(slab > 0, value, jnp.zeros_like(value))
 
     def link(d, row, column):
         return coupling[2] * depth_ref[d, row : row + 1, column : column + 1]
 
     def with_edges(edge, ends_value, v_first, v_own):
         row = 0 if edge == 0 else size - 1
-        return ends_value + 2.0 * v_own + (2.0 * coupling[2] * corner * link(slab, row, 0)) * v_first
+        return ends_value + 2.0 * v_own + (2.0 * coupling[2] * corner() * link(slab, row, 0)) * v_first
 
     @named("early")
     def early_edges():
@@ -508,15 +521,49 @@
     def early(k):
         return remote(
             ends, gathered.at[slab], early_send.at[k - 1], early_recv.at[k - 1],
-            lax.rem(slab + k, slabs), "slab",
-        )
-
-    def last_link(k):
+            {"slab": lax.rem(slab + k, slabs)},
+        )
+
+    def late_own(k):
         return remote(
-            late.at[pl.ds(0, 4)], late_in.at[slab, pl.ds(0, 4)],
-            late_send.at[k - 1], late_recv.at[k - 1],
-            lax.rem(slab + k, slabs), "slab",
-        )
+            late.at[pl.ds(0, 6)], late_in.at[x, slab, pl.ds(0, 6)],
+            own_send.at[k - 1], own_recv.at[k - 1], {"slab": lax.rem(slab + k, slabs)},
+        )
+
+    def late_cross(k):
+        return remote(
+            late.at[pl.ds(8, 6)], late_in.at[x, slab, pl.ds(0, 6)],
+            cross_send.at[k], cross_recv.at[k],
+            {"pencil": pair, "slab": lax.rem(slab + k, slabs)},
+        )
+
+    @named("late_edges")
+    def late_edges():
+        for who in range(2):
+            for side in range(2):
+                if who == 0:
+                    plane = final[side, pl.ds(pl.multiple_of(x * seg, 8), half)]
+                    rows = final[side, pl.ds(pl.multiple_of(x * seg + half, 8), extra)]
+                else:
+                    plane = back_out[side, pl.ds(0, half)]
+                    rows = back_out[side, pl.ds(half, extra)]
+                lines = dot(at_ends[...], both(plane, 1), ((1,), (1,)))
+                first, last = lines[0:1] + lines[2:3], lines[1:2] + lines[3:4]
+                v_last, v_first = (
+                    jnp.concatenate(
+                        [rows[2 * strip + k : 2 * strip + k + 1] for strip in range(strips)], axis=1
+                    )
+                    for k in (0, 1)
+                )
+                row = 8 * who + side
+                late[row : row + 1] = with_edges(0, first, v_first, v_first)
+                late[row + 2 : row + 3] = with_edges(1, last, v_first, v_last)
+                late[row + 4 : row + 5] = v_first
+        for k in range(1, slabs):
+            late_own(k).start()
+        for k in range(slabs):
+            late_cross(k).start()
+        late_in[x, slab, 0:6] = late[0:6]
 
     def chain(first_of, last_of, v_first):
         zero = jnp.zeros_like(v_first)
@@ -532,97 +579,74 @@
         for d in range(1, slabs):
             carry_in = jnp.where(slab == d, forward[d], carry_in)
             carry_next = jnp.where(slab == d, backward[d], carry_next)
-        return carry_in + (2.0 * coupling[2] * corner) * v_first, carry_next
+        return carry_in + (2.0 * coupling[2] * corner()) * v_first, carry_next
 
     reach = lag * (outer - 1)
-    ticks = max(chunks + reach, groups + 2)
-    ready = (chunks + 1) // 2
+    settle = 3
+    heavy = chunks
+    ticks = max(settle + chunks + reach, heavy + groups + 1)
 
     def tick(t, unused):
-        @pl.when(t < 2)
-        def _():
-            def ours(c, same):
-                whole_chunk(1, x, c)
-                return same
-
-            lax.fori_loop(t * ready, jnp.minimum(t * ready + ready, chunks - 1), ours, 0)
-
-        @pl.when(t == 1)
+        @pl.when(t < chunks - 1)
+        def _():
+            whole_chunk(0, 1 - x, t)
+
+        @pl.when(t == chunks - 1)
+        def _():
+            last_chunk(0, 1 - x)
+
+        @pl.when(t == 0)
+        def _():
+            pl.semaphore_wait(barrier, 3 + 2 * (slabs - 1))
+
+        @pl.when(t < chunks)
+        def _():
+            to_pair(t).start()
+
+        @pl.when((t >= 1) & (t < chunks))
+        def _():
+            whole_chunk(1, x, t - 1)
+
+        @pl.when(t == chunks)
         def _():
             last_chunk(1, x)
-
-        @pl.when(t < chunks)
-        def _():
-            do_pair(t)
-
-        up = t - lag * z
+            prepare()
+
+        @pl.when((t >= settle) & (t < settle + chunks))
+        def _():
+            do_pair(t - settle)
+
+        up = t - settle - lag * z
+        down = t - settle - lag * (outer - 1 - z)
+        done = t - settle - lag * jnp.maximum(z, outer - 1 - z)
 
         @pl.when((up >= 0) & (up < chunks))
         def _():
             do_up(up)
 
-        down = t - lag * (outer - 1 - z)
-
         @pl.when((down >= 0) & (down < chunks))
         def _():
             do_down(down)
 
-        done = t - lag * jnp.maximum(z, outer - 1 - z)
-
         @pl.when((done >= 0) & (done < chunks))
         def _():
             do_final(done)
 
-        @pl.when((t >= 1) & (t <= groups))
-        def _():
-            solve_planes(t - 1)
-
-        @pl.when(t == groups + 1)
+        @pl.when(done == chunks - 1)
+        def _():
+            late_edges()
+
+        @pl.when((t >= heavy) & (t < heavy + groups))
+        def _():
+            solve_planes(t - heavy)
+
+        @pl.when(t == heavy + groups)
         def _():
             early_edges()
 
         return unused
 
     lax.fori_loop(0, ticks, tick, 0)
-
-    @named("back")
-    def wait_back(c, unused):
-        to_back(c).wait()
-        return unused
-
-    lax.fori_loop(0, chunks, wait_back, 0)
-    with jax.named_scope("late_solve"):
-        rhs = jnp.concatenate(
-            [
-                jnp.concatenate([final[side, blocks_at(i)] for i in range(count)], axis=0)
-                for side in range(2)
-            ],
-            axis=1,
-        )
-        answers = solve_group(rhs, coupling[0], width_ref, mixed_ref, mixed_depth[...])
-        pieces = []
-        for i in range(count):
-            h, strip = i // strips, i % strips
-            rows = [
-                final[side, h * seg + half + 2 * strip + 1 - edge, :].reshape(1, depth)
-                for edge in (0, 1) for side in (0, 1)
-            ]
-            rows.append(jnp.zeros((4, depth), F32))
-            pieces.append(jnp.concatenate(rows, axis=0))
-        value = jnp.concatenate(rows_solve(pieces, coupling[0], width_ref, mixed_ref), axis=1)
-        edges = jnp.where(lax.div(lane, 2) == 0, pltpu.roll(answers[0], 1, 1), pltpu.roll(answers[1], 3, 1))
-        z_edges[...] = edges
-        lines = [turn_rows(z_edges, i, 2) for i in range(count)]
-        lines = [jnp.concatenate([line[edge] for line in lines], axis=1) for edge in (0, 1)]
-        for edge in range(2):
-            for side in range(2):
-                own = value[edge * 2 + side : edge * 2 + side + 1]
-                late[edge * 2 + side : edge * 2 + side + 1] = with_edges(
-                    edge, lines[edge][side : side + 1], value[side : side + 1], own
-                )
-    for k in range(1, slabs):
-        last_link(k).start()
-    late_in[slab, 0:4] = late[0:4]
 
     with jax.named_scope("early_wait"):
         for k in range(1, slabs):
@@ -658,23 +682,45 @@
         return unused
 
     lax.fori_loop(0, groups, finish_planes, 0)
+    @named("back")
+    def wait_back(c, unused):
+        to_back(c).wait()
+        return unused
+
+    lax.fori_loop(0, chunks, wait_back, 0)
+    with jax.named_scope("late_depth"):
+        for side in range(2):
+            rows = jnp.concatenate([final[side, blocks_at(i)] for i in range(count)], axis=0)
+            face_ref[side] = depth_solve(rows, mixed_depth)
+
     with jax.named_scope("late_wait"):
         for k in range(1, slabs):
-            last_link(k).wait()
-    carry_in, carry_next = chain(
-        lambda d: late_in[d, 0:2], lambda d: late_in[d, 2:4], value[0:2]
-    )
-    pieces = []
-    for side in range(2):
-        (a_high, a_low), (b_high, b_low) = split(carry_in[side : side + 1]), split(carry_next[side : side + 1])
-        pieces += [a_high, a_low, a_high, b_high, b_low, b_high]
-    six = (in_high, in_high, in_low, next_high, next_high, next_low)
-    blank = jnp.zeros((1, depth), F32)
-    row_pairs = [jnp.concatenate([piece.astype(F32), blank], axis=1) for piece in six]
-    row_pairs += [jnp.concatenate([blank, piece.astype(F32)], axis=1) for piece in six]
-    spread = dot(rows_of(pieces, width), rows_of(row_pairs, 2 * depth), ((0,), (0,)))
-    for side in range(2):
-        face_ref[side] = answers[side] + spread[:, side * depth : (side + 1) * depth]
+            late_own(k).wait()
+        for k in range(slabs):
+            late_cross(k).wait()
+
+    def late_rows(d, row):
+        return jnp.concatenate([late_in[h, d, row : row + 2] for h in range(2)], axis=1)
+
+    with jax.named_scope("late_chain"):
+        carry_in, carry_next = chain(
+            lambda d: late_rows(d, 0), lambda d: late_rows(d, 2), late_rows(slab, 4)
+        )
+        pieces = []
+        for side in range(2):
+            (a_high, a_low), (b_high, b_low) = split(carry_in[side : side + 1]), split(carry_next[side : side + 1])
+            pieces += [a_high, a_low, a_high, b_high, b_low, b_high]
+        six = (in_high, in_high, in_low, next_high, next_high, next_low)
+        blank = jnp.zeros((1, depth), F32)
+        row_pairs = [jnp.concatenate([piece.astype(F32), blank], axis=1) for piece in six]
+        row_pairs += [jnp.concatenate([blank, piece.astype(F32)], axis=1) for piece in six]
+        spread = dot(rows_of(pieces, width), rows_of(row_pairs, 2 * depth), ((0,), (0,)))
+
+    with jax.named_scope("late_solve"):
+        sides = [face_ref[side] + spread[:, side * depth : (side + 1) * depth] for side in range(2)]
+        solved = width_solve(jnp.concatenate(sides, axis=1), coupling[0], width_ref, mixed_ref)
+        for side in range(2):
+            face_ref[side] = solved[:, side * depth : (side + 1) * depth]
 
     @named("sent")
     def wait_sent(c, unused):
@@ -723,7 +769,7 @@
     planes, width, depth = density.shape
     pencils, slabs = lax.axis_size("pencil"), lax.axis_size("slab")
     blocks, size = width_inverse.shape[:2]
-    group = 2
+    group = 4
     half = width // 2
     extra = -(-2 * half // depth // 8) * 8
     seg = half + extra
@@ -740,8 +786,9 @@
     two = pltpu.VMEM((2, seg, depth), F32)
     steps = dma((chunks,))
     peers = dma((slabs - 1,))
+    operands = (coupling, density, source, width_inverse, depth_inverse)
     z, face, table = pl.pallas_call(
-        lambda *refs: step_kernel(group, pencils, slabs, chunk, 2, *refs),
+        lambda *refs: step_kernel(group, pencils, slabs, chunk, 3, *refs),
         out_shape=(field, faces, table),
         in_specs=[far, far, far, far, far],
         out_specs=(vmem, vmem, vmem),
@@ -754,6 +801,8 @@
             pltpu.VMEM((planes, 2 * seg, depth), F32),
             pltpu.VMEM((blocks, 2 * size, 2 * size), BF16),
             pltpu.VMEM((2 * size, 2 * size), BF16),
+            pltpu.VMEM((2 * depth, 2 * depth), BF16),
+            pltpu.VMEM((16, 2 * depth), BF16),
             pltpu.VMEM((width, depth), F32),
             pltpu.VMEM((width, depth), F32),
             pltpu.VMEM((blocks, 2 * planes, depth), F32),
@@ -763,16 +812,16 @@
             pltpu.VMEM((2, planes, width), F32),
             pltpu.VMEM((slabs, 2, planes, width), F32),
             pltpu.VMEM((2, planes, width), F32),
-            pltpu.VMEM((8, width), F32),
-            pltpu.VMEM((slabs, 8, width), F32),
+            pltpu.VMEM((16, half), F32),
+            pltpu.VMEM((2, slabs, 8, half), F32),
             dma((4 + 4 * (half // depth),)), dma((3,)),
             steps, steps, steps, steps, steps, steps, steps, steps,
-            peers, peers, peers, peers,
+            peers, peers, peers, peers, dma((slabs,)), dma((slabs,)),
         ],
         compiler_params=pltpu.CompilerParams(
             vmem_limit_bytes=44 * 1024 * 1024, collective_id=0, has_side_effects=True
         ),
-    )(coupling, density, source, width_inverse, depth_inverse)
+    )(*[pltpu.with_memory_space_constraint(array, pltpu.HBM) for array in operands])
 
     parts = 8
     return pl.pallas_call(

time: 42.7 us -> 34.9 us (0.82)
  Pallas kernels: 39.9 us -> 34.8 us
  local copies, waits for them, and re-layouts: 2.6 us -> 0 us
    pallas_call x1, Pallas kernels: 37 us -> 31.9 us  [per_device(): pl.pallas_call(lambda *refs: step_kernel(group, pencils, slabs, chunk, 3,...]
    unnamed x6 -> x0, local copies, waits for them, and re-layouts: 2.6 us -> none
where the time goes in v3:
time: 34.9 us; the launch traced here: 34.8 us
  Pallas kernels  34.8 us (100%)
    pallas_call x1, Pallas kernels, per_device(): pl.pallas_call(lambda *refs: step_kernel(group, pencils, slabs, chunk, 3,...  31.9 us
    pallas_call x1, Pallas kernels, per_device(): pl.pallas_call(lambda *refs: finish_kernel(parts, *refs), out_shape=field...  2.84 us

profile of v3, /device:TPU:0, one launch (start us, length us, event | category | flops | bytes accessed | tf_op | source)
XLA Modules:
  0.0 34.8 jit_solution(18042689602339777134)
XLA Ops:
  0.0 31.9 %shard_map.55 = (f32[16,768,128]{2,1,0:T(8,128)S(1)}, f32[2,768,128]{2,1,0:T(8,128)S(1)}, f32[16,128]{1,0:T(8,128)S(1)}) custom-call(f32[3]{0:T(128)} %refs_0_.1, f32[16,768,128]{2,1,0:T(8,128)} %refs_1_.1, f32[16,768,128]{2,1,0:T(8,128)} %refs_2_.1, f32[6,128,128]{2,1,0:T(8,128)} %refs_3_.1, f32[4,128,128]{2,1,0:T(8,128)} %refs_4_.1), custom_call_target="tpu_custom_call" | custom-call | tf_op jit(solution)/shard_map/pallas_call | solution.py:790
  31.9 2.8 %shard_map.56 = f32[16,768,128]{2,1,0:T(8,128)} custom-call(f32[16,768,128]{2,1,0:T(8,128)S(1)} %get-tuple-element.8.refs_0_, f32[2,768,128]{2,1,0:T(8,128)S(1)} %get-tuple-element.9.refs_1_, f32[16,128]{1,0:T(8,128)S(1)} %get-tuple-element.10.refs_2_), custom_call_target="tpu_custom_call" | custom-call | tf_op jit(solution)/shard_map/pallas_call | solution.py:827

commit v4 on v3

--- a/solution.py
+++ b/solution.py
@@ -132,7 +132,7 @@
     z_ref, face_ref, coef_ref,
     coupling, width_ref, depth_ref,
     rho_ref, source_ref, y_ref, mixed_ref, mixed_depth,
-    shifts, at_ends, rho_edges, z_edges, turned, columns,
+    shifts, at_ends, links, rho_edges, z_edges, turned, columns,
     pair_out, pair_in, block, up_out, up_in, down_out, down_in, back_out, final,
     ends, gathered, carries, late, late_in,
     load_sem, table_sem, pair_send, pair_recv, up_send, up_recv, down_send, down_recv,
@@ -146,17 +146,30 @@
     extra = seg - half
     chunks = seg // chunk
     strips = half // depth
+    step = depth // 2
+    cuts = half // step
     pad = 8
     me, slab = lax.axis_index("pencil"), lax.axis_index("slab")
     outer = pencils // 2
     z, x = lax.div(me, 2), lax.rem(me, 2)
     pair = z * 2 + 1 - x
+    bottom, top = z == 0, z == outer - 1
+    inside = (z > 0) & (z < outer - 1)
+    gives_more = (bottom & (x == 0)) | (top & (x == 1))
     above_me = lax.rem(me + 2, pencils)
     below_me = lax.rem(me + pencils - 2, pencils)
 
     barrier = pltpu.get_barrier_semaphore()
-    for peer in (pair, above_me, below_me):
-        pl.semaphore_signal(barrier, inc=1, device_id={"pencil": peer}, device_id_type=MESH)
+    pl.semaphore_signal(barrier, inc=1, device_id={"pencil": pair}, device_id_type=MESH)
+
+    @pl.when(z < outer - 1)
+    def _():
+        pl.semaphore_signal(barrier, inc=1, device_id={"pencil": above_me}, device_id_type=MESH)
+
+    @pl.when(z > 0)
+    def _():
+        pl.semaphore_signal(barrier, inc=1, device_id={"pencil": below_me}, device_id_type=MESH)
+
     for k in range(1, slabs):
         peer = lax.rem(slab + k, slabs)
         for whom in ({"slab": peer}, {"pencil": pair, "slab": peer}):
@@ -177,13 +190,13 @@
         return load(("rim", h, side), rho_hbm, rho_ref, start, 8, pad)
 
     def main(turn, h, piece):
-        low = 8 if piece == 0 else piece * depth
-        high = half - 8 if piece == strips - 1 else (piece + 1) * depth
+        low = 8 if piece == 0 else piece * step
+        high = half - 8 if piece == cuts - 1 else (piece + 1) * step
         return load(("rho", turn, piece), rho_hbm, rho_ref, h * half + low, high - low, pad)
 
     def other(turn, h, piece):
-        start = h * half + piece * depth
-        return load(("source", turn, piece), source_hbm, source_ref, start, depth, 0)
+        start = h * half + piece * step
+        return load(("source", turn, piece), source_hbm, source_ref, start, step, 0)
 
     tables = [
         pltpu.make_async_copy(src, dst, table_sem.at[k])
@@ -195,7 +208,7 @@
     for h in (0, 1):
         for side in (0, 1):
             rim(h, side).start()
-    for piece in range(strips):
+    for piece in range(cuts):
         for turn, h in ((0, 1 - x), (1, x)):
             main(turn, h, piece).start()
             other(turn, h, piece).start()
@@ -317,21 +330,44 @@
             down_out.at[at], down_in.at[at], down_send.at[c], down_recv.at[c], below_me
         )
 
-    def to_back(c):
+    def to_back(c, slots):
         return remote(
-            back_out.at[:, rows_at(c)], final.at[:, rows_at(c, x * seg)],
+            back_out.at[slots, rows_at(c)], final.at[slots, rows_at(c, x * seg)],
             back_send.at[c], back_recv.at[c], pair,
         )
 
+    def each_back(act):
+        @pl.when(inside)
+        def _():
+            act(pl.ds(0, 2))
+
+        @pl.when(bottom)
+        def _():
+            act(pl.ds(1, 1))
+
+        @pl.when(top)
+        def _():
+            act(pl.ds(0, 1))
+
     def keep(turn, at, faces):
+        first, last = faces
         if turn == 0:
-            pair_out[0, at], pair_out[1, at] = faces
-
-    need = [min(strips, -(-(c * chunk + chunk + 1) // depth)) for c in range(chunks)]
-    first_use = [next(c for c in range(chunks) if need[c] > piece) for piece in range(strips)]
+            pair_out[0, at] = first
+            pair_out[1, at] = last
+        else:
+            @pl.when(bottom & (x == 0))
+            def _():
+                pair_out[0, at] = last
+
+            @pl.when(top & (x == 1))
+            def _():
+                pair_out[1, at] = first
+
+    need = [min(cuts, -(-(c * chunk + chunk + 1) // step)) for c in range(chunks)]
+    first_use = [next(c for c in range(chunks) if need[c] > piece) for piece in range(cuts)]
 
     def whole_chunk(turn, h, c):
-        for piece in range(strips):
+        for piece in range(cuts):
             @pl.when(c == first_use[piece])
             def _():
                 main(turn, h, piece).wait()
@@ -341,7 +377,7 @@
         keep(turn, pl.ds(row, chunk), sweep(h, row, chunk))
 
     def last_chunk(turn, h):
-        for piece in range(strips):
+        for piece in range(cuts):
             if first_use[piece] == chunks - 1:
                 main(turn, h, piece).wait()
                 other(turn, h, piece).wait()
@@ -362,6 +398,22 @@
             mixed_ref[i, :size, size:] = high
             mixed_ref[i, size:, :size] = low
             mixed_ref[i, size:, size:] = jnp.zeros_like(low)
+        def spot(d, row, column):
+            return depth_ref[d, row : row + 1, column : column + 1]
+
+        for d in range(slabs):
+            for k, (row, column) in enumerate(((0, 0), (0, size - 1), (size - 1, 0))):
+                value = coupling[2] * spot(d, row, column)
+                links[3 * d + k : 3 * d + k + 1] = jnp.broadcast_to(value, (1, depth))
+        corner = spot(jnp.where(slab > 0, slab - 1, 0), size - 1, size - 1)
+        corner = 2.0 * coupling[2] * jnp.where(slab > 0, corner, jnp.zeros_like(corner))
+        for k, value in enumerate(
+            (
+                corner, corner * coupling[2] * spot(slab, 0, 0),
+                corner * coupling[2] * spot(slab, size - 1, 0),
+            )
+        ):
+            links[3 * slabs + k : 3 * slabs + k + 1] = jnp.broadcast_to(value, (1, depth))
         first_high, first_low = split(depth_ref[slab, 0:1])
         last_high, last_low = split(depth_ref[slab, size - 1 : size])
         nothing = jnp.zeros((1, depth), F32)
@@ -452,7 +504,7 @@
         final[1, mine] = jnp.where(lower, inner_high, leave)
         back_out[0, at] = jnp.where(lower, inner_low, enter)
         back_out[1, at] = jnp.where(lower, leave, inner_high)
-        to_back(c).start()
+        each_back(lambda slots: to_back(c, slots).start())
 
     def blocks_at(i):
         return pl.ds(i // strips * seg + i % strips * size, size)
@@ -487,16 +539,14 @@
         turned[i] = source[pl.ds(i * size, size)].T[: turned.shape[1]]
         return [turned[i, pl.ds(edge, rows, stride=2)] for edge in (1, 0)]
 
-    def corner():
-        value = depth_ref[jnp.where(slab > 0, slab - 1, 0), size - 1 : size, size - 1 : size]
-        return jnp.where(slab > 0, value, jnp.zeros_like(value))
-
     def link(d, row, column):
-        return coupling[2] * depth_ref[d, row : row + 1, column : column + 1]
+        return like(3 * d + 2 * (row > 0) + (column > 0))
+
+    def like(number, lanes=width):
+        return jnp.concatenate([links[number : number + 1]] * (lanes // depth), axis=1)
 
     def with_edges(edge, ends_value, v_first, v_own):
-        row = 0 if edge == 0 else size - 1
-        return ends_value + 2.0 * v_own + (2.0 * coupling[2] * corner() * link(slab, row, 0)) * v_first
+        return ends_value + 2.0 * v_own + like(3 * slabs + 1 + (edge > 0), v_first.shape[1]) * v_first
 
     @named("early")
     def early_edges():
@@ -579,11 +629,11 @@
         for d in range(1, slabs):
             carry_in = jnp.where(slab == d, forward[d], carry_in)
             carry_next = jnp.where(slab == d, backward[d], carry_next)
-        return carry_in + (2.0 * coupling[2] * corner()) * v_first, carry_next
+        return carry_in + like(3 * slabs) * v_first, carry_next
 
     reach = lag * (outer - 1)
     settle = 3
-    heavy = chunks
+    heavy = chunks - 1
     ticks = max(settle + chunks + reach, heavy + groups + 1)
 
     def tick(t, unused):
@@ -597,38 +647,52 @@
 
         @pl.when(t == 0)
         def _():
-            pl.semaphore_wait(barrier, 3 + 2 * (slabs - 1))
-
-        @pl.when(t < chunks)
+            @pl.when(inside)
+            def _():
+                pl.semaphore_wait(barrier, 3 + 2 * (slabs - 1))
+
+            @pl.when(jnp.logical_not(inside))
+            def _():
+                pl.semaphore_wait(barrier, 2 + 2 * (slabs - 1))
+
+        @pl.when((t < chunks) & jnp.logical_not(gives_more))
         def _():
             to_pair(t).start()
 
-        @pl.when((t >= 1) & (t < chunks))
-        def _():
-            whole_chunk(1, x, t - 1)
-
-        @pl.when(t == chunks)
+        @pl.when(t < chunks - 1)
+        def _():
+            whole_chunk(1, x, t)
+
+        @pl.when(t == chunks - 1)
         def _():
             last_chunk(1, x)
             prepare()
 
+        @pl.when((t < chunks) & gives_more)
+        def _():
+            to_pair(t).start()
+
         @pl.when((t >= settle) & (t < settle + chunks))
         def _():
             do_pair(t - settle)
 
-        up = t - settle - lag * z
-        down = t - settle - lag * (outer - 1 - z)
-        done = t - settle - lag * jnp.maximum(z, outer - 1 - z)
-
-        @pl.when((up >= 0) & (up < chunks))
+        def chunk_after(hops):
+            number = t - settle - lag * hops
+            return jnp.where(number < chunks, number, -1)
+
+        up = chunk_after(z)
+        down = chunk_after(outer - 1 - z)
+        done = chunk_after(jnp.maximum(z, outer - 1 - z))
+
+        @pl.when(up >= 0)
         def _():
             do_up(up)
 
-        @pl.when((down >= 0) & (down < chunks))
+        @pl.when(down >= 0)
         def _():
             do_down(down)
 
-        @pl.when((done >= 0) & (done < chunks))
+        @pl.when(done >= 0)
         def _():
             do_final(done)
 
@@ -651,6 +715,7 @@
     with jax.named_scope("early_wait"):
         for k in range(1, slabs):
             early(k).wait()
+    wide = 4
     in_row = coupling[2] * depth_ref[slab, 0:1]
     next_row = coupling[2] * depth_ref[slab, size - 1 : size]
     (in_high, in_low), (next_high, next_low) = split(in_row), split(next_row)
@@ -674,24 +739,50 @@
 
     @named("fix")
     def finish_planes(index, unused):
-        j = index * group
-        rhs = jnp.concatenate([jnp.where(spot == j + g, base, 0.0) for g in range(group)], axis=1)
+        j = index * wide
+        rhs = jnp.concatenate([jnp.where(spot == j + g, base, 0.0) for g in range(wide)], axis=1)
         both_planes = dot(columns[...], rhs.astype(BF16), ((1,), (0,)))
-        for g in range(group):
+        for g in range(wide):
             z_ref[j + g] = z_ref[j + g] + both_planes[:, g * depth : (g + 1) * depth]
         return unused
 
-    lax.fori_loop(0, groups, finish_planes, 0)
+    lax.fori_loop(0, planes // wide, finish_planes, 0)
+    def depth_part(h):
+        for side in range(2):
+            rows = final[side, pl.ds(pl.multiple_of(h * seg, 8), half)]
+            to = pl.ds(pl.multiple_of(h * half, 8), half)
+            face_ref[side, to] = depth_solve(rows, mixed_depth)
+
+    depth_part(x)
+
     @named("back")
     def wait_back(c, unused):
-        to_back(c).wait()
+        each_back(lambda slots: to_back(c, slots).wait())
+        at, theirs = rows_at(c), rows_at(c, (1 - x) * seg)
+
+        @pl.when(bottom & (x == 0))
+        def _():
+            final[0, theirs] = jnp.zeros((chunk, depth), F32)
+
+        @pl.when(bottom & (x == 1))
+        def _():
+            leave = y_ref[0, theirs] + far * final[1, theirs]
+            final[0, theirs] = gain * (pair_in[0, at] + near * leave)
+
+        @pl.when(top & (x == 0))
+        def _():
+            enter = y_ref[planes - 1, theirs] + far * final[0, theirs]
+            final[1, theirs] = gain * (pair_in[1, at] + near * enter)
+
+        @pl.when(top & (x == 1))
+        def _():
+            final[1, theirs] = jnp.zeros((chunk, depth), F32)
+
         return unused
 
     lax.fori_loop(0, chunks, wait_back, 0)
     with jax.named_scope("late_depth"):
-        for side in range(2):
-            rows = jnp.concatenate([final[side, blocks_at(i)] for i in range(count)], axis=0)
-            face_ref[side] = depth_solve(rows, mixed_depth)
+        depth_part(1 - x)
 
     with jax.named_scope("late_wait"):
         for k in range(1, slabs):
@@ -769,7 +860,7 @@
     planes, width, depth = density.shape
     pencils, slabs = lax.axis_size("pencil"), lax.axis_size("slab")
     blocks, size = width_inverse.shape[:2]
-    group = 4
+    group = 2
     half = width // 2
     extra = -(-2 * half // depth // 8) * 8
     seg = half + extra
@@ -788,7 +879,7 @@
     peers = dma((slabs - 1,))
     operands = (coupling, density, source, width_inverse, depth_inverse)
     z, face, table = pl.pallas_call(
-        lambda *refs: step_kernel(group, pencils, slabs, chunk, 3, *refs),
+        lambda *refs: step_kernel(group, pencils, slabs, chunk, 4, *refs),
         out_shape=(field, faces, table),
         in_specs=[far, far, far, far, far],
         out_specs=(vmem, vmem, vmem),
@@ -803,6 +894,7 @@
             pltpu.VMEM((2 * size, 2 * size), BF16),
             pltpu.VMEM((2 * depth, 2 * depth), BF16),
             pltpu.VMEM((16, 2 * depth), BF16),
+            pltpu.VMEM((-(-(3 * slabs + 3) // 8) * 8, depth), F32),
             pltpu.VMEM((width, depth), F32),
             pltpu.VMEM((width, depth), F32),
             pltpu.VMEM((blocks, 2 * planes, depth), F32),
@@ -814,7 +906,7 @@
             pltpu.VMEM((2, planes, width), F32),
             pltpu.VMEM((16, half), F32),
             pltpu.VMEM((2, slabs, 8, half), F32),
-            dma((4 + 4 * (half // depth),)), dma((3,)),
+            dma((4 + 8 * (half // depth),)), dma((3,)),
             steps, steps, steps, steps, steps, steps, steps, steps,
             peers, peers, peers, peers, dma((slabs,)), dma((slabs,)),
         ],

time: 34.9 us -> 33.8 us (0.968)
  Pallas kernels: 34.8 us -> 33.6 us
    pallas_call x1, Pallas kernels: 31.9 us -> 30.8 us  [per_device(): pl.pallas_call(lambda *refs: step_kernel(group, pencils, slabs, chunk, 4,...]
where the time goes in v4:
time: 33.8 us; the launch traced here: 33.7 us
  Pallas kernels  33.6 us (99%)
    pallas_call x1, Pallas kernels, per_device(): pl.pallas_call(lambda *refs: step_kernel(group, pencils, slabs, chunk, 4,...  30.8 us
    pallas_call x1, Pallas kernels, per_device(): pl.pallas_call(lambda *refs: finish_kernel(parts, *refs), out_shape=field...  2.84 us

profile of v4, /device:TPU:0, one launch (start us, length us, event | category | flops | bytes accessed | tf_op | source)
XLA Modules:
  0.0 33.7 jit_solution(7520024927634255406)
XLA Ops:
  0.0 30.8 %shard_map.55 = (f32[16,768,128]{2,1,0:T(8,128)S(1)}, f32[2,768,128]{2,1,0:T(8,128)S(1)}, f32[16,128]{1,0:T(8,128)S(1)}) custom-call(f32[3]{0:T(128)} %refs_0_.1, f32[16,768,128]{2,1,0:T(8,128)} %refs_1_.1, f32[16,768,128]{2,1,0:T(8,128)} %refs_2_.1, f32[6,128,128]{2,1,0:T(8,128)} %refs_3_.1, f32[4,128,128]{2,1,0:T(8,128)} %refs_4_.1), custom_call_target="tpu_custom_call" | custom-call | tf_op jit(solution)/shard_map/pallas_call | solution.py:881
  30.8 2.8 %shard_map.56 = f32[16,768,128]{2,1,0:T(8,128)} custom-call(f32[16,768,128]{2,1,0:T(8,128)S(1)} %get-tuple-element.8.refs_0_, f32[2,768,128]{2,1,0:T(8,128)S(1)} %get-tuple-element.9.refs_1_, f32[16,128]{1,0:T(8,128)S(1)} %get-tuple-element.10.refs_2_), custom_call_target="tpu_custom_call" | custom-call | tf_op jit(solution)/shard_map/pallas_call | solution.py:919

commit v5 on v4

--- a/solution.py
+++ b/solution.py
@@ -137,6 +137,7 @@
     ends, gathered, carries, late, late_in,
     load_sem, table_sem, pair_send, pair_recv, up_send, up_recv, down_send, down_recv,
     back_send, back_recv, early_send, early_recv, own_send, own_recv, cross_send, cross_recv,
+    more_send, more_recv,
 ):
     planes, width, depth = z_ref.shape
     groups = planes // group
@@ -155,7 +156,7 @@
     pair = z * 2 + 1 - x
     bottom, top = z == 0, z == outer - 1
     inside = (z > 0) & (z < outer - 1)
-    gives_more = (bottom & (x == 0)) | (top & (x == 1))
+    outside = jnp.logical_not(inside)
     above_me = lax.rem(me + 2, pencils)
     below_me = lax.rem(me + pencils - 2, pencils)
 
@@ -208,11 +209,11 @@
     for h in (0, 1):
         for side in (0, 1):
             rim(h, side).start()
-    for piece in range(cuts):
-        for turn, h in ((0, 1 - x), (1, x)):
+    for turn, h in ((0, 1 - x), (1, x)):
+        for piece in range(cuts):
             main(turn, h, piece).start()
             other(turn, h, piece).start()
-        if piece == 0:
+        if turn == 0:
             tables[1].start()
             tables[2].start()
 
@@ -314,11 +315,39 @@
     def rows_at(c, shift=0):
         return pl.ds(pl.multiple_of(c * chunk + shift, 8), chunk)
 
-    def to_pair(c):
+    def to_pair(c, slots):
         at = rows_at(c)
         return remote(
-            pair_out.at[:, at], pair_in.at[:, at], pair_send.at[c], pair_recv.at[c], pair
-        )
+            pair_out.at[slots, at], pair_in.at[slots, at], pair_send.at[c], pair_recv.at[c], pair
+        )
+
+    def to_pair_later(c, slots):
+        at = rows_at(c)
+        return remote(
+            pair_out.at[slots, at], pair_in.at[slots, at], more_send.at[c], more_recv.at[c], pair
+        )
+
+    def each_pair(act):
+        @pl.when(inside)
+        def _():
+            act(pl.ds(0, 2))
+
+        @pl.when(bottom)
+        def _():
+            act(pl.ds(1, 1))
+
+        @pl.when(top)
+        def _():
+            act(pl.ds(0, 1))
+
+    def each_more(act):
+        @pl.when(bottom)
+        def _():
+            act(pl.ds(0, 1))
+
+        @pl.when(top)
+        def _():
+            act(pl.ds(1, 1))
 
     def to_above(c):
         at = rows_at(c)
@@ -354,6 +383,14 @@
         if turn == 0:
             pair_out[0, at] = first
             pair_out[1, at] = last
+
+            @pl.when(bottom & (x == 1))
+            def _():
+                pair_out[1, at] = last + far * gain * near * first
+
+            @pl.when(top & (x == 0))
+            def _():
+                pair_out[0, at] = first + far * gain * near * last
         else:
             @pl.when(bottom & (x == 0))
             def _():
@@ -441,25 +478,38 @@
     def _():
         down_in[...] = jnp.zeros_like(down_in)
 
-    def faces_of(c):
+    @pl.when(outside)
+    def _():
+        block[...] = jnp.zeros_like(block)
+
+    @named("pair")
+    def do_pair(c):
+        each_pair(lambda slots: to_pair(c, slots).wait_recv())
         at, mine = rows_at(c), rows_at(c, x * seg)
         own_first, own_last = y_ref[0, mine], y_ref[planes - 1, mine]
-        its_first, its_last = pair_in[0, at], pair_in[1, at]
         lower = x == 0
-        return (
-            jnp.where(lower, own_first, its_first),
-            jnp.where(lower, own_last, its_last),
-            jnp.where(lower, its_first, own_first),
-            jnp.where(lower, its_last, own_last),
-        )
-
-    @named("pair")
-    def do_pair(c):
-        to_pair(c).wait_recv()
-        at = rows_at(c)
-        f0, l0, f1, l1 = faces_of(c)
-        block[0, at] = f0 + far * gain * (f1 + near * l0)
-        block[1, at] = l1 + far * gain * (l0 + near * f1)
+
+        @pl.when(inside)
+        def _():
+            its_first, its_last = pair_in[0, at], pair_in[1, at]
+            f0, l0 = jnp.where(lower, own_first, its_first), jnp.where(lower, own_last, its_last)
+            f1, l1 = jnp.where(lower, its_first, own_first), jnp.where(lower, its_last, own_last)
+            block[0, at] = f0 + far * gain * (f1 + near * l0)
+            block[1, at] = l1 + far * gain * (l0 + near * f1)
+
+        @pl.when(bottom)
+        def _():
+            its = pair_in[1, at]
+            block[1, at] = jnp.where(
+                lower, its + far * gain * own_last, own_last + far * gain * (its + near * own_first)
+            )
+
+        @pl.when(top)
+        def _():
+            its = pair_in[0, at]
+            block[0, at] = jnp.where(
+                lower, own_first + far * gain * (its + near * own_last), its + far * gain * own_first
+            )
 
     @named("up")
     def do_up(c):
@@ -494,9 +544,9 @@
         high = down_in[at] + over * block[1, at]
         enter = k_uu * low + k_uo * high
         leave = k_ou * low + k_oo * high
-        f0, l0, f1, l1 = faces_of(c)
-        l0 = l0 + far * enter
-        f1 = f1 + far * leave
+        each_more(lambda slots: to_pair_later(c, slots).wait_recv())
+        l0 = jnp.where(x == 0, y_ref[planes - 1, mine], pair_in[1, at]) + far * enter
+        f1 = jnp.where(x == 0, pair_in[0, at], y_ref[0, mine]) + far * leave
         inner_low = gain * (l0 + near * f1)
         inner_high = gain * (f1 + near * l0)
         lower = x == 0
@@ -631,72 +681,86 @@
             carry_next = jnp.where(slab == d, backward[d], carry_next)
         return carry_in + like(3 * slabs) * v_first, carry_next
 
-    reach = lag * (outer - 1)
-    settle = 3
+    n = chunks - 1
+    turn_tick = (n + 1) // 2
+    first_pair = turn_tick + 2
+    pairs = (chunks + 1) // 2
     heavy = chunks - 1
-    ticks = max(settle + chunks + reach, heavy + groups + 1)
+    ticks = max(first_pair + lag * (outer - 1) + pairs, heavy + groups + 1)
 
     def tick(t, unused):
-        @pl.when(t < chunks - 1)
-        def _():
-            whole_chunk(0, 1 - x, t)
-
-        @pl.when(t == chunks - 1)
+        def for_pair(c, same):
+            whole_chunk(0, 1 - x, c)
+
+            @pl.when(c == 0)
+            def _():
+                @pl.when(inside)
+                def _():
+                    pl.semaphore_wait(barrier, 3 + 2 * (slabs - 1))
+
+                @pl.when(outside)
+                def _():
+                    pl.semaphore_wait(barrier, 2 + 2 * (slabs - 1))
+
+            each_pair(lambda slots: to_pair(c, slots).start())
+            return same
+
+        def for_us(c, same):
+            whole_chunk(1, x, c)
+            return same
+
+        lax.fori_loop(jnp.minimum(2 * t, n), jnp.minimum(2 * t + 2, n), for_pair, 0)
+
+        @pl.when(t == turn_tick)
         def _():
             last_chunk(0, 1 - x)
-
-        @pl.when(t == 0)
-        def _():
-            @pl.when(inside)
-            def _():
-                pl.semaphore_wait(barrier, 3 + 2 * (slabs - 1))
-
-            @pl.when(jnp.logical_not(inside))
-            def _():
-                pl.semaphore_wait(barrier, 2 + 2 * (slabs - 1))
-
-        @pl.when((t < chunks) & jnp.logical_not(gives_more))
-        def _():
-            to_pair(t).start()
-
-        @pl.when(t < chunks - 1)
-        def _():
-            whole_chunk(1, x, t)
-
-        @pl.when(t == chunks - 1)
+            each_pair(lambda slots: to_pair(n, slots).start())
+
+        ours = 2 * (t - turn_tick)
+        lax.fori_loop(jnp.clip(ours - 1, 0, n), jnp.clip(ours + 1, 0, n), for_us, 0)
+
+        @pl.when(t == turn_tick + n // 2)
         def _():
             last_chunk(1, x)
             prepare()
 
-        @pl.when((t < chunks) & gives_more)
-        def _():
-            to_pair(t).start()
-
-        @pl.when((t >= settle) & (t < settle + chunks))
-        def _():
-            do_pair(t - settle)
-
-        def chunk_after(hops):
-            number = t - settle - lag * hops
-            return jnp.where(number < chunks, number, -1)
-
-        up = chunk_after(z)
-        down = chunk_after(outer - 1 - z)
-        done = chunk_after(jnp.maximum(z, outer - 1 - z))
-
-        @pl.when(up >= 0)
-        def _():
-            do_up(up)
-
-        @pl.when(down >= 0)
-        def _():
-            do_down(down)
-
-        @pl.when(done >= 0)
-        def _():
-            do_final(done)
-
-        @pl.when(done == chunks - 1)
+            def more(c, same):
+                each_more(lambda slots: to_pair_later(c, slots).start())
+                return same
+
+            lax.fori_loop(0, chunks, more, 0)
+
+        rel = t - first_pair
+        low = jnp.where(rel < 2, 2 * rel, rel + 1)
+        high = low + jnp.where(rel < 2, 2, jnp.where(rel == 2, 0, 1))
+
+        @pl.when(inside)
+        def _():
+            def one_pair(c, same):
+                do_pair(c)
+                return same
+
+            lax.fori_loop(jnp.clip(low, 0, chunks), jnp.clip(high, 0, chunks), one_pair, 0)
+
+        def in_twos(hops, act):
+            number = 2 * (t - first_pair - lag * hops)
+
+            def one(c, same):
+                act(c)
+                return same
+
+            lax.fori_loop(jnp.clip(number, 0, chunks), jnp.clip(number + 2, 0, chunks), one, 0)
+            return number
+
+        @pl.when(outside)
+        def _():
+            in_twos(0, do_pair)
+
+        in_twos(z, do_up)
+        in_twos(outer - 1 - z, do_down)
+        most = in_twos(jnp.maximum(z, outer - 1 - z), do_final)
+
+        @pl.when((most < chunks) & (most + 2 >= chunks))
         def _():
             late_edges()
 
@@ -815,7 +879,8 @@
 
     @named("sent")
     def wait_sent(c, unused):
-        to_pair(c).wait_send()
+        each_pair(lambda slots: to_pair(c, slots).wait_send())
+        each_more(lambda slots: to_pair_later(c, slots).wait_send())
 
         @pl.when(z < outer - 1)
         def _():
@@ -879,7 +944,7 @@
     peers = dma((slabs - 1,))
     operands = (coupling, density, source, width_inverse, depth_inverse)
     z, face, table = pl.pallas_call(
-        lambda *refs: step_kernel(group, pencils, slabs, chunk, 4, *refs),
+        lambda *refs: step_kernel(group, pencils, slabs, chunk, 3, *refs),
         out_shape=(field, faces, table),
         in_specs=[far, far, far, far, far],
         out_specs=(vmem, vmem, vmem),
@@ -908,7 +973,7 @@
             pltpu.VMEM((2, slabs, 8, half), F32),
             dma((4 + 8 * (half // depth),)), dma((3,)),
             steps, steps, steps, steps, steps, steps, steps, steps,
-            peers, peers, peers, peers, dma((slabs,)), dma((slabs,)),
+            peers, peers, peers, peers, dma((slabs,)), dma((slabs,)), steps, steps,
         ],
         compiler_params=pltpu.CompilerParams(
             vmem_limit_bytes=44 * 1024 * 1024, collective_id=0, has_side_effects=True

time: 33.8 us -> 33.8 us (level)
  no operation moved by 1% of the time
where the time goes in v5:
time: 33.8 us; the launch traced here: 33.5 us
  Pallas kernels  33.5 us (99%)
    pallas_call x1, Pallas kernels, per_device(): pl.pallas_call(lambda *refs: step_kernel(group, pencils, slabs, chunk, 3,...  30.7 us
    pallas_call x1, Pallas kernels, per_device(): pl.pallas_call(lambda *refs: finish_kernel(parts, *refs), out_shape=field...  2.84 us

profile of v5, /device:TPU:0, one launch (start us, length us, event | category | flops | bytes accessed | tf_op | source)
XLA Modules:
  0.0 33.5 jit_solution(17636881065681761720)
XLA Ops:
  0.0 30.7 %shard_map.55 = (f32[16,768,128]{2,1,0:T(8,128)S(1)}, f32[2,768,128]{2,1,0:T(8,128)S(1)}, f32[16,128]{1,0:T(8,128)S(1)}) custom-call(f32[3]{0:T(128)} %refs_0_.1, f32[16,768,128]{2,1,0:T(8,128)} %refs_1_.1, f32[16,768,128]{2,1,0:T(8,128)} %refs_2_.1, f32[6,128,128]{2,1,0:T(8,128)} %refs_3_.1, f32[4,128,128]{2,1,0:T(8,128)} %refs_4_.1), custom_call_target="tpu_custom_call" | custom-call | tf_op jit(solution)/shard_map/pallas_call | solution.py:946
  30.7 2.8 %shard_map.56 = f32[16,768,128]{2,1,0:T(8,128)} custom-call(f32[16,768,128]{2,1,0:T(8,128)S(1)} %get-tuple-element.8.refs_0_, f32[2,768,128]{2,1,0:T(8,128)S(1)} %get-tuple-element.9.refs_1_, f32[16,128]{1,0:T(8,128)S(1)} %get-tuple-element.10.refs_2_), custom_call_target="tpu_custom_call" | custom-call | tf_op jit(solution)/shard_map/pallas_call | solution.py:984

commit v6 on v4

--- a/solution.py
+++ b/solution.py
@@ -915,7 +915,7 @@
         ),
     )(*[pltpu.with_memory_space_constraint(array, pltpu.HBM) for array in operands])
 
-    parts = 8
+    parts = 16
     return pl.pallas_call(
         lambda *refs: finish_kernel(parts, *refs),
         out_shape=field,

time: 33.8 us -> 33.8 us (level)
  no operation moved by 1% of the time
where the time goes in v6:
time: 33.8 us; the launch traced here: 33.6 us
  Pallas kernels  33.6 us (99%)
    pallas_call x1, Pallas kernels, per_device(): pl.pallas_call(lambda *refs: step_kernel(group, pencils, slabs, chunk, 4,...  30.8 us
    pallas_call x1, Pallas kernels, per_device(): pl.pallas_call(lambda *refs: finish_kernel(parts, *refs), out_shape=field...  2.83 us

profile of v6, /device:TPU:0, one launch (start us, length us, event | category | flops | bytes accessed | tf_op | source)
XLA Modules:
  0.0 33.6 jit_solution(5967419227926009314)
XLA Ops:
  0.0 30.8 %shard_map.55 = (f32[16,768,128]{2,1,0:T(8,128)S(1)}, f32[2,768,128]{2,1,0:T(8,128)S(1)}, f32[16,128]{1,0:T(8,128)S(1)}) custom-call(f32[3]{0:T(128)} %refs_0_.1, f32[16,768,128]{2,1,0:T(8,128)} %refs_1_.1, f32[16,768,128]{2,1,0:T(8,128)} %refs_2_.1, f32[6,128,128]{2,1,0:T(8,128)} %refs_3_.1, f32[4,128,128]{2,1,0:T(8,128)} %refs_4_.1), custom_call_target="tpu_custom_call" | custom-call | tf_op jit(solution)/shard_map/pallas_call | solution.py:881
  30.8 2.8 %shard_map.56 = f32[16,768,128]{2,1,0:T(8,128)} custom-call(f32[16,768,128]{2,1,0:T(8,128)S(1)} %get-tuple-element.8.refs_0_, f32[2,768,128]{2,1,0:T(8,128)S(1)} %get-tuple-element.9.refs_1_, f32[16,128]{1,0:T(8,128)S(1)} %get-tuple-element.10.refs_2_), custom_call_target="tpu_custom_call" | custom-call | tf_op jit(solution)/shard_map/pallas_call | solution.py:919
